TPU v7x, 32 devices: a whole 2x2x4 slice. The times are simulated.
32 devices in a mesh: gx: 4 (over y, x), gy: 2 (over core), gz: 4 (over z).
Axes of the slice: x: 2, y: 2, z: 4, core: 2. Of those that a mesh axis runs over, the one named last changes fastest.
Arguments:
- old_pos: float32 [3, 4, 2, 4, 1536], P(None, 'gx', 'gy', 'gz'), may hold values from -6 to 6
- displacement: float32 [3, 4, 2, 4, 1536], P(None, 'gx', 'gy', 'gz'), may hold values from -0.3 to 0.3
- inv_mass: float32 [4, 2, 4, 1536], P('gx', 'gy', 'gz'), may hold values from 0.0625 to 1
- bond_head: int32 [4, 2, 4, 1024], P('gx', 'gy', 'gz'), may hold values from 0 to 1535, as said below
- bond_tail: int32 [4, 2, 4, 1024], P('gx', 'gy', 'gz'), may hold values from 0 to 1967, as said below
- send_list: int32 [4, 2, 4, 16], P('gx', 'gy', 'gz'), may hold values from 0 to 1535, as said below
Outputs:
- new_pos: float32 [3, 4, 2, 4, 1536], P(None, 'gx', 'gy', 'gz')
- multipliers: float32 [4, 2, 4, 1024], P('gx', 'gy', 'gz')
Inputs may be any that keep to these rules, and one draw needn't show every extreme that they name: `bond_head`: distinct atoms of the owning domain; no atom is the first atom of two constraints. `bond_tail`: below 1536: an atom of the owning domain other than the constraint's first atom, never in send_list; otherwise a slot 1536 + block * 16 + entry with block in 0..26 other than 13, distinct within a domain; 192 constraints of each domain use such slots. `send_list`: distinct atoms of the domain; a send atom is never a constraint's first atom and never a local second atom.
All inputs are finite; a program needn't handle non-finite values.
Results may differ from a plain program's by a relative error of at most 0.0011.
Values sent between devices are 32-bit elements; how exact they have to be, the bound alone decides.
A program may use at most 64 MiB of HBM per device.

v0:
```python
import functools
import itertools

import jax
import jax.numpy as jnp
from jax import lax
from jax.experimental import pallas as pl
from jax.experimental.pallas import tpu as pltpu
from jax.sharding import PartitionSpec as P

ORDER = 4
LANES = 128
F32, BF16 = jnp.float32, jnp.bfloat16
MESH = pl.DeviceIdType.MESH


def pieces(value):
    high = value.astype(BF16).astype(F32)
    rest = value - high
    middle = rest.astype(BF16).astype(F32)
    return jnp.concatenate([high, middle, rest - middle], axis=0).astype(BF16)


def fold(out):
    rows = out.shape[0] // 3
    return out[:rows] + out[rows : 2 * rows] + out[2 * rows :]


def dot_nt(left, right):
    return lax.dot_general(left, right, (((1,), (1,)), ((), ())), preferred_element_type=F32)


def dot_nn(left, right):
    return lax.dot_general(left, right, (((1,), (0,)), ((), ())), preferred_element_type=F32)


def rows8(parts):
    count = sum(part.shape[0] for part in parts)
    pad = -count % 8
    if pad:
        parts = list(parts) + [jnp.zeros((pad, parts[0].shape[1]), F32)]
    return jnp.concatenate(parts, axis=0)


def plan(sizes, send_count):
    groups = LANES // send_count
    entries = []
    for block in range(27):
        off = (block // 9 - 1, block // 3 % 3 - 1, block % 3 - 1)
        if off == (0, 0, 0):
            continue
        canon = tuple(o % n for o, n in zip(off, sizes))
        for where, blocks in entries:
            if where == canon and all((b - block) % groups for b in blocks):
                blocks.append(block)
                break
        else:
            entries.append((canon, [block]))
    return entries


def kernel(
    axes, sizes, send_count,
    old_ref, move_ref, mass_ref, head_ref, tail_ref, send_ref,
    pos_ref, mult_ref,
    low, pick, above, beside, root, col,
    out0, in0, out1, in1, out2, in2, out3, in3, out4, in4,
    send_sem, recv_sem,
):
    atoms = old_ref.shape[-1]
    bonds = head_ref.shape[-1]
    groups = LANES // send_count
    slot_tiles = -(-27 // groups)
    slots = slot_tiles * LANES
    entries = plan(sizes, send_count)
    devices = []
    for where, _ in entries:
        if where != (0, 0, 0) and where not in devices:
            devices.append(where)
    here = [lax.axis_index(name) for name in axes]

    def target(where):
        return tuple(lax.rem(i + o, n) for i, o, n in zip(here, where, sizes))

    barrier = pltpu.get_barrier_semaphore()
    for where in devices:
        pl.semaphore_signal(barrier, inc=1, device_id=target(where), device_id_type=MESH)

    send_row = jnp.concatenate(
        [send_ref[0, 0].astype(F32), jnp.zeros((1, LANES - send_count), F32)], axis=1
    )
    send_rep = jnp.broadcast_to(send_row, (8, LANES))
    shift = send_count
    while shift < LANES:
        send_rep = send_rep + pltpu.roll(send_rep, shift, 1)
        shift *= 2
    send_col = send_rep.T[:, 0:1]
    atom_lane = lax.broadcasted_iota(jnp.int32, (1, atoms), 1).astype(F32)
    pick[...] = jnp.where(send_col == atom_lane, 1.0, 0.0).astype(BF16)

    old = jnp.concatenate([old_ref[k, 0, 0] for k in range(3)], axis=0)
    pos0 = old + jnp.concatenate([move_ref[k, 0, 0] for k in range(3)], axis=0)
    mass = mass_ref[0, 0]
    data = rows8([old, pos0, mass])
    out0[...] = fold(dot_nt(pieces(data), pick[...]))

    if devices:
        pl.semaphore_wait(barrier, len(devices))

    def copies_same(step, source, landing):
        started = []
        for i, where in enumerate(devices):
            copy = pltpu.make_async_remote_copy(
                source, landing.at[i], send_sem.at[step, i], recv_sem.at[step, i],
                device_id=target(where), device_id_type=MESH,
            )
            copy.start()
            started.append(copy)
        return started

    def copies_each(step, source, landing):
        started = []
        for i, (where, _) in enumerate(entries):
            if where == (0, 0, 0):
                landing[i] = source[i]
                continue
            copy = pltpu.make_async_remote_copy(
                source.at[i], landing.at[i], send_sem.at[step, i], recv_sem.at[step, i],
                device_id=target(where), device_id_type=MESH,
            )
            copy.start()
            started.append(copy)
        return started

    pending = []

    def arrive(started):
        for copy in started:
            copy.wait_recv()
        pending.extend(started)

    lane_group = lax.broadcasted_iota(jnp.int32, (1, LANES), 1) // send_count

    def view(own, landing):
        tiles = []
        for q in range(slot_tiles):
            tile = jnp.zeros(own.shape, F32)
            for block in range(q * groups, min(27, (q + 1) * groups)):
                if block == 13:
                    continue
                off = (block // 9 - 1, block // 3 % 3 - 1, block % 3 - 1)
                back = tuple(-o % n for o, n in zip(off, sizes))
                data = own[...] if back == (0, 0, 0) else landing[devices.index(back)]
                tile = jnp.where(lane_group == block % groups, data, tile)
            tiles.append(tile)
        return jnp.concatenate(tiles, axis=1)

    def fill(source, rows):
        for i, (_, blocks) in enumerate(entries):
            tile = jnp.zeros((rows.shape[0], LANES), F32)
            for block in blocks:
                q = block // groups
                tile = jnp.where(
                    lane_group == block % groups, rows[:, q * LANES : (q + 1) * LANES], tile
                )
            source[i] = tile

    first = copies_same(0, out0, in0)

    head = head_ref[0, 0].astype(F32)
    tail = tail_ref[0, 0].astype(F32)
    end_atom = jnp.concatenate([head_ref[0, 0], tail_ref[0, 0]], axis=1)
    end_tile = (end_atom // LANES).astype(F32)
    end_lane = (end_atom % LANES).astype(F32)
    col[...] = rows8([head, tail, end_lane[:, :bonds], end_lane[:, bonds:]]).T
    one_lane = lax.broadcasted_iota(jnp.int32, (1, LANES), 1).astype(F32)
    atom_tiles = atoms // LANES
    step_rows = 16

    def index_rows(i, carry):
        base = pl.multiple_of(i * step_rows, step_rows)
        block = col[pl.ds(base, step_rows), :]
        h, t = block[:, 0:1], block[:, 1:2]
        low[pl.ds(base, step_rows), :] = jnp.where(block[:, 2:3] == one_lane, 1.0, 0.0).astype(BF16)
        low[pl.ds(bonds + base, step_rows), :] = jnp.where(
            block[:, 3:4] == one_lane, 1.0, 0.0
        ).astype(BF16)
        above[pl.ds(base, step_rows), :] = jnp.where(t == head, 1.0, 0.0).astype(BF16)
        beside[pl.ds(base, step_rows), :] = jnp.where(
            t == tail, 1.0, jnp.where(h == tail, -1.0, 0.0)
        ).astype(BF16)
        return carry

    lax.fori_loop(0, bonds // step_rows, index_rows, 0)

    def take(rows, hot, where, base):
        tiles = rows.shape[1] // LANES
        stacked = jnp.concatenate(
            [rows[:, k * LANES : (k + 1) * LANES] for k in range(tiles)], axis=0
        )
        found = fold(dot_nt(pieces(stacked), hot))
        total = jnp.zeros((8, hot.shape[0]), F32)
        for k in range(tiles):
            total = jnp.where(where == base + k, found[8 * k : 8 * k + 8], total)
        return total

    at_ends = take(data, low[...], end_tile, 0)
    is_far = tail >= atoms
    flags = jnp.where(is_far, 1.0, 0.0)

    def climb(label):
        rows = jnp.broadcast_to(label, (8, bonds))
        high = rows.astype(BF16).astype(F32)
        both = jnp.concatenate([high, rows - high], axis=0).astype(BF16)
        out = dot_nt(both, above[...])
        return jnp.where(is_far, tail, out[0:1] + out[8:9])

    def mark(label):
        col[:, 0:8] = jnp.broadcast_to(label, (8, bonds)).T
        slot_lane = (lax.broadcasted_iota(jnp.int32, (1, slots), 1) + atoms).astype(F32)

        def mark_rows(i, carry):
            base = pl.multiple_of(i * 32, 32)
            block = col[pl.ds(base, 32), :]
            root[pl.ds(base, 32), :] = jnp.where(block[:, 0:1] == slot_lane, 1.0, 0.0).astype(BF16)
            return carry

        lax.fori_loop(0, bonds // 32, mark_rows, 0)

    label = jnp.where(is_far, tail, 0.0)
    for _ in range(ORDER // 2):
        label = climb(label)
    mark(label)

    arrive(first)
    at_tail = at_ends[:, bonds:] + take(
        view(out0, in0), low[bonds:, :], end_tile[:, bonds:], atom_tiles
    )
    apart = at_ends[:, :bonds] - at_tail
    mass_head, mass_tail = at_ends[6:7, :bonds], at_tail[6:7]
    bond_old = apart[0:3]
    bond_new = apart[3:6]
    length = jnp.maximum(jnp.sqrt(jnp.sum(bond_old * bond_old, axis=0, keepdims=True)), 0.5)
    direction = bond_old / length
    scale = 1.0 / jnp.sqrt(mass_head + mass_tail)
    bent = scale * direction
    near_mass = jnp.where(is_far, 0.0, mass_tail)
    right1 = scale * (jnp.sum(direction * bond_new, axis=0, keepdims=True) - length)

    def meet(pull):
        rows = rows8([pull])
        count = rows.shape[0]
        high = rows.astype(BF16).astype(F32)
        both = jnp.concatenate([high, rows - high], axis=0).astype(BF16)
        up = dot_nn(both, above[...])
        side = dot_nn(both, beside[...])
        out = mass_head * (rows - up[:count] - up[count:]) + near_mass * (side[:count] + side[count:])
        return out[: pull.shape[0]]

    def couple(*rows):
        out = meet(jnp.concatenate([bent * row for row in rows], axis=0))
        return [
            row - jnp.sum(bent * out[3 * k : 3 * k + 3], axis=0, keepdims=True)
            for k, row in enumerate(rows)
        ]

    def to_slots(rows):
        return fold(dot_nn(pieces(rows8(rows)), root[...]))

    def to_bonds(rows):
        return fold(dot_nt(pieces(rows8(rows)), root[...]))

    mass_send = out0[6:7, :]

    def owner(terms, normal, response):
        moved, answers = [], []
        for k in range(ORDER + 1):
            here_k = terms[k]
            for i in range(k):
                gap = k - 1 - i
                here_k = here_k + (answers[i] if gap == 0 else response[gap - 1] * answers[i])
            total = rows8([jnp.sum(n * here_k, axis=0, keepdims=True) for n in normal])
            shift = send_count
            while shift < LANES:
                total = total + pltpu.roll(total, shift, 1)
                shift *= 2
            total = -mass_send * total
            moved.append(total[0:3])
            answers.append(sum(normal[d] * total[d : d + 1] for d in range(3)))
        return moved

    def through(injected):
        total = 0.0
        weight = 0.0
        for k in range(ORDER):
            weight = weight + far_terms[k]
            total = total + weight * injected[ORDER - 1 - k : ORDER - k]
        return total

    terms1, far_terms = [right1], [flags]
    half = ORDER // 2
    for _ in range(half):
        near, far = couple(terms1[-1], far_terms[-1])
        terms1.append(near)
        far_terms.append(far)

    def at_far(terms, k):
        return far_terms[max(0, k - half)] * terms[min(k, half)]

    fixed = to_slots([bent * flags] + [at_far(far_terms, k) for k in range(1, ORDER)])
    own_terms = to_slots([at_far(terms1, k) for k in range(ORDER + 1)])
    fill(out1, jnp.concatenate([fixed, own_terms], axis=0))
    second = copies_each(1, out1, in1)

    def longer(steps, label):
        for _ in range(steps):
            near, far = couple(terms1[-1], far_terms[-1])
            terms1.append(near)
            far_terms.append(far)
            label = climb(label)
        return label

    label = longer((ORDER - half) // 2, label)
    arrive(second)
    normal = [in1[:, k, :] for k in range(3)]
    response = [in1[:, 3 + k, :] for k in range(ORDER - 1)]
    moved1 = owner([in1[:, 8 + k, :] for k in range(ORDER + 1)], normal, response)
    sum1 = sum(moved1[1:], moved1[0])
    out2[...] = rows8(moved1[:ORDER] + [sum1])
    third = copies_same(2, out2, in2)
    mark(longer(ORDER - half - (ORDER - half) // 2, label))
    base1 = sum(terms1[1:], terms1[0])
    arrive(third)

    def answer(rows):
        return [
            sum(fixed[d : d + 1] * rows[3 * k + d : 3 * k + d + 1] for d in range(3))
            for k in range(ORDER)
        ]

    seen = view(out2, in2)
    injected = to_bonds(answer(seen) + [seen[3 * ORDER : 3 * ORDER + 3]])
    sol1 = base1 + through(injected)
    stretch = bond_new - (meet(bent * sol1) - flags * injected[ORDER : ORDER + 3])
    current = jnp.sum(stretch * stretch, axis=0, keepdims=True)
    square = length * length
    goal = jnp.sqrt(jnp.maximum(2.0 * square - current, 0.5 * square))
    right2 = scale * (length - goal)
    fill(out3, to_slots([far_terms[k] * right2 for k in range(ORDER + 1)]))
    fourth = copies_each(3, out3, in3)
    term, both = right2, sol1 + right2
    for _ in range(half):
        (term,) = couple(term)
        both = both + term
    arrive(fourth)
    moved2 = owner([in3[:, k, :] for k in range(ORDER + 1)], normal, response)
    sum2 = sum(moved2[1:], moved2[0])
    out4[...] = rows8(moved2[:ORDER])
    fifth = copies_same(4, out4, in4)
    for _ in range(ORDER - half):
        (term,) = couple(term)
        both = both + term
    once = jnp.where(lane_group == 0, sum1 + sum2, 0.0)
    start = pos0 - fold(dot_nn(pieces(rows8([once])), pick[...]))[0:3]
    arrive(fifth)
    both = both + through(to_bonds(answer(view(out4, in4))))
    mult_ref[0, 0] = both
    pull = bent * both
    parts = pieces(rows8([jnp.concatenate([pull, -pull], axis=1)])).astype(F32)
    kept = jnp.concatenate(
        [jnp.where(end_tile == k, parts, 0.0) for k in range(atom_tiles)], axis=0
    )
    added = dot_nn(kept.astype(BF16), low[...])
    added = jnp.concatenate(
        [fold(added[24 * k : 24 * k + 24]) for k in range(atom_tiles)], axis=1
    )
    result = start - mass * added[0:3]
    for k in range(3):
        pos_ref[k, 0, 0] = result[k : k + 1]
    for copy in pending:
        copy.wait_send()


def per_device(axes, sizes, old_pos, displacement, inv_mass, bond_head, bond_tail, send_list):
    atoms, bonds, send_count = old_pos.shape[-1], bond_head.shape[-1], send_list.shape[-1]
    groups = LANES // send_count
    slots = -(-27 // groups) * LANES
    entries = plan(sizes, send_count)
    count = max(1, len(entries))
    same = max(1, len({where for where, _ in entries} - {(0, 0, 0)}))
    tile = lambda *shape: pltpu.VMEM(shape + (LANES,), F32)
    return pl.pallas_call(
        functools.partial(kernel, axes, sizes, send_count),
        out_shape=(
            jax.ShapeDtypeStruct(old_pos.shape, F32),
            jax.ShapeDtypeStruct(bond_head.shape, F32),
        ),
        in_specs=[pl.BlockSpec(memory_space=pltpu.VMEM)] * 6,
        out_specs=(pl.BlockSpec(memory_space=pltpu.VMEM), pl.BlockSpec(memory_space=pltpu.VMEM)),
        scratch_shapes=[
            pltpu.VMEM((2 * bonds, LANES), BF16),
            pltpu.VMEM((LANES, atoms), BF16),
            pltpu.VMEM((bonds, bonds), BF16),
            pltpu.VMEM((bonds, bonds), BF16),
            pltpu.VMEM((bonds, slots), BF16),
            pltpu.VMEM((bonds, 8), F32),
            tile(8), tile(same, 8),
            tile(count, 16), tile(count, 16),
            tile(16), tile(same, 16),
            tile(count, 8), tile(count, 8),
            tile(16), tile(same, 16),
            pltpu.SemaphoreType.DMA((5, count)),
            pltpu.SemaphoreType.DMA((5, count)),
        ],
        compiler_params=pltpu.CompilerParams(
            collective_id=0, has_side_effects=True, vmem_limit_bytes=56 * 1024 * 1024
        ),
    )(old_pos, displacement, inv_mass, bond_head, bond_tail, send_list)


def solution(mesh):
    axes = ("gx", "gy", "gz")
    sizes = tuple(mesh.shape[name] for name in axes)
    return jax.shard_map(
        functools.partial(per_device, axes, sizes),
        mesh=mesh,
        in_specs=(
            P(None, "gx", "gy", "gz", None),
            P(None, "gx", "gy", "gz", None),
            P("gx", "gy", "gz", None),
            P("gx", "gy", "gz", None),
            P("gx", "gy", "gz", None),
            P("gx", "gy", "gz", None),
        ),
        out_specs=(P(None, "gx", "gy", "gz", None), P("gx", "gy", "gz", None)),
        check_vma=False,
    )
```

profile of v0, /device:TPU:0, one launch (start us, length us, event | category | flops | bytes accessed | tf_op | source)
XLA Modules:
  0.0 50.5 jit_solution(14873629037271392048)
XLA Ops:
  0.6 47.9 %shard_map.77 = (f32[3,1,1,1,1536]{4,3,2,1,0:T(1,128)}, f32[1,1,1,1024]{3,2,1,0:T(1,128)}) custom-call(f32[3,1,1,1,1536]{4,3,2,1,0:T(1,128)} %old_ref.1, f32[3,1,1,1,1536]{4,3,2,1,0:T(1,128)} %move_ref.1, f32[1,1,1,1536]{3,2,1,0:T(1,128)} %mass_ref.1, s32[1,1,1,1024]{3,2,1,0:T(1,128)} %head_ref.1, s32[1,1,1,1024]{3,2,1,0:T(1,128)} %tail_ref.1, ...), custom_call_target="tpu_custom_call" | custom-call | tf_op jit(solution)/shard_map/pallas_call | solution.py:392
  48.5 0.0 copy-start
  48.5 1.3 %copy.10 = f32[3,1,1,1,1536]{4,3,2,1,0:T(1,128)} copy(f32[3,1,1,1,1536]{4,3,2,1,0:T(1,128)} %get-tuple-element.4) | data formatting | bytes 36864
  49.9 0.0 copy-done
  49.9 0.6 %copy.11 = f32[1,1,1,1024]{3,2,1,0:T(1,128)} copy(f32[1,1,1,1024]{3,2,1,0:T(1,128)S(1)} %copy-done) | data formatting | bytes 8192
Async XLA Ops:
  48.5 1.3 %copy-start = (f32[1,1,1,1024]{3,2,1,0:T(1,128)S(1)}, f32[1,1,1,1024]{3,2,1,0:T(1,128)}, u32[]{:S(2)}) copy-start(f32[1,1,1,1024]{3,2,1,0:T(1,128)} %get-tuple-element.5) | copy-start | bytes 12292
where the time goes:
time: 50.7 us; the launch traced here: 50.5 us
  Pallas kernels  47.9 us (94%)
  local copies, waits for them, and re-layouts  1.93 us (4%)
  between operations  0.65 us (1%)
    pallas_call x1, Pallas kernels, per_device(): pl.pallas_call(functools.partial(kernel, axes, sizes, send_count), out_sh...  47.9 us
    unnamed x4, local copies, waits for them, and re-layouts  1.93 us

commit v1 on v0

v1 whole, which is shorter than its diff:
```python
import functools

import jax
import jax.numpy as jnp
from jax import lax
from jax.experimental import pallas as pl
from jax.experimental.pallas import tpu as pltpu
from jax.sharding import PartitionSpec as P

ORDER = 4
LANES = 128
SUBS = 8
F32, BF16, I32 = jnp.float32, jnp.bfloat16, jnp.int32
MESH = pl.DeviceIdType.MESH
SYM = ((0, 0), (0, 1), (0, 2), (1, 1), (1, 2), (2, 2))


def dot_nt(left, right):
    return lax.dot_general(left, right, (((1,), (1,)), ((), ())), preferred_element_type=F32)


def dot_nn(left, right):
    return lax.dot_general(left, right, (((1,), (0,)), ((), ())), preferred_element_type=F32)


def wide(row, count=SUBS):
    return jnp.broadcast_to(row, (count, row.shape[1]))


def lanes_at(rows, index):
    return jnp.take_along_axis(rows, index, axis=1, mode="promise_in_bounds")


def subs_at(rows, index):
    return jnp.take_along_axis(rows, index, axis=0, mode="promise_in_bounds")


def split(value):
    high = value.astype(BF16).astype(F32)
    return high, value - high


def flips(n):
    return n >= 4 and n % 2 == 0


def routes(sizes):
    classes = [(a, b, c) for a in range(3) for b in range(3) for c in range(3)]
    direct, forth, back = [], [], []
    for cls in classes:
        direct.append(tuple((1 - c) for c in cls))
        forth.append(tuple((0, 1, -2)[c] if flips(n) else c - 1 for c, n in zip(cls, sizes)))
        back.append(tuple((0, 1, 2)[c] if flips(n) else 1 - c for c, n in zip(cls, sizes)))
    return classes, direct, forth, back


def kernel(
    axes, sizes, send_count,
    old_ref, move_ref, mass_ref, head_ref, tail_ref, send_ref,
    pos_ref, mult_ref,
    table, hot_head, hot_tail, hot_root, mask_tail, mask_root, stage,
    out0, in0, out1, in1, out2, in2, out3, in3, out4, in4,
    send_sem, recv_sem,
):
    atoms, bonds = old_ref.shape[-1], head_ref.shape[-1]
    atom_rows, bond_rows = atoms // LANES, bonds // LANES
    slot_rows = bond_rows + -(-(atoms - bonds) // LANES)
    width = send_count
    bits = width.bit_length() - 1
    classes, direct, forth, back = routes(sizes)
    centre = classes.index((1, 1, 1))
    hub_row = classes.index(tuple(0 if flips(n) else 1 for n in sizes))
    tiles = -(-len(classes) // SUBS)
    here = [lax.axis_index(name) for name in axes]
    turn = [1 - 2 * lax.rem(i, 2) if flips(n) else 1 for i, n in zip(here, sizes)]

    def nowhere(offset):
        return all(o % n == 0 for o, n in zip(offset, sizes))

    def target(offset):
        return tuple(
            lax.rem(i + o * s + 2 * n, n) for i, o, s, n in zip(here, offset, turn, sizes)
        )

    greet = []
    for group in (direct, forth, back):
        for offset in group:
            key = tuple(o % n for o, n in zip(offset, sizes))
            if any(key) and key not in [k for k, _ in greet]:
                greet.append((key, offset))
    barrier = pltpu.get_barrier_semaphore()
    for _, offset in greet:
        pl.semaphore_signal(barrier, inc=1, device_id=target(offset), device_id_type=MESH)

    sub = lax.broadcasted_iota(I32, (SUBS, LANES), 0)
    lane = lax.broadcasted_iota(I32, (SUBS, LANES), 1)
    group = lax.shift_right_logical(lane, bits)
    entry = lane & (width - 1)
    swap = (group - sub) & (SUBS - 1)
    unskew = (lane + width * sub) & (LANES - 1)

    def transpose8(x):
        x = pltpu.roll(x, 0, 1, stride=width, stride_axis=0)
        return lanes_at(subs_at(x, swap), unskew)

    def pick_rows(choice):
        index = jnp.zeros((SUBS, LANES), I32)
        for j, c in enumerate(choice):
            if c:
                index = jnp.where(sub == j, c, index)
        return index

    old = [old_ref[k, 0, 0].reshape(atom_rows, LANES) for k in range(3)]
    pos0 = [old[k] + move_ref[k, 0, 0].reshape(atom_rows, LANES) for k in range(3)]
    mass = mass_ref[0, 0].reshape(atom_rows, LANES)
    values = old + pos0 + [mass, jnp.zeros((atom_rows, LANES), F32)]
    for g, value in enumerate(values):
        for q in range(atom_rows):
            table[SUBS * q + g : SUBS * q + g + 1, :] = value[q : q + 1]
    send_row = jnp.concatenate(
        [send_ref[0, 0], jnp.zeros((1, LANES - send_count), I32)], axis=1
    )
    send_rep = lanes_at(wide(send_row), entry)
    send_tile, send_lane = lax.shift_right_logical(send_rep, 7), send_rep & (LANES - 1)
    found = jnp.zeros((SUBS, LANES), F32)
    for q in range(atom_rows):
        found = jnp.where(
            send_tile == q, lanes_at(table[SUBS * q : SUBS * q + SUBS, :], send_lane), found
        )
    found = jnp.sum(jnp.where(group == sub, found, 0.0), axis=0, keepdims=True)
    out0[0] = wide(found)
    for land in (in1, in3):
        for part in range(land.shape[0]):
            land[part, centre : centre + 1, :] = jnp.zeros((1, LANES), F32)
            land[part, len(classes) :, :] = jnp.zeros((SUBS * tiles - len(classes), LANES), F32)

    pl.semaphore_wait(barrier, len(greet))

    order = sorted(range(len(classes)), key=lambda r: -(classes[r][0] + classes[r][2]))

    def copies(step, source, landing, offsets, each, whole):
        started = []
        for row in order:
            if row == centre and not whole:
                continue
            line = row if each else 0
            if nowhere(offsets[row]):
                landing[:, row : row + 1, :] = source[:, line : line + 1, :]
                continue
            copy = pltpu.make_async_remote_copy(
                source.at[:, line], landing.at[:, row],
                send_sem.at[step, row], recv_sem.at[step, row],
                device_id=target(offsets[row]), device_id_type=MESH,
            )
            copy.start()
            started.append(copy)
        return started

    pending = []

    def arrive(started):
        for copy in started:
            copy.wait_recv()
        pending.extend(started)

    first = copies(0, out0, in0, direct, False, False)

    head = head_ref[0, 0].reshape(bond_rows, LANES)
    tail = tail_ref[0, 0].reshape(bond_rows, LANES)
    head_tile, head_lane = lax.shift_right_logical(head, 7), head & (LANES - 1)
    tail_tile, tail_lane = lax.shift_right_logical(tail, 7), tail & (LANES - 1)
    is_far = tail >= atoms
    slot = jnp.maximum(tail - atoms, 0)
    block = lax.shift_right_logical(slot, bits)
    one = lambda test: jnp.where(test, 1, 0)
    bx = one(block >= 9) + one(block >= 18)
    rest = block - 9 * bx
    by = one(rest >= 3) + one(rest >= 6)
    bz = rest - 3 * by
    place = [
        1 - s * (b - 1) if flips(n) else b
        for b, s, n in zip((bx, by, bz), turn, sizes)
    ]
    slot = ((place[0] * 3 + place[1]) * 3 + place[2]) * width + (slot & (width - 1))

    def gather(rows, tile, index, start=0.0, count=None):
        shape = index.shape
        total = jnp.full(shape, start, rows.dtype)
        for q in range(count or rows.shape[0]):
            total = jnp.where(tile == q, lanes_at(wide(rows[q : q + 1], shape[0]), index), total)
        return total

    deep = lax.broadcasted_iota(I32, (LANES, LANES), 0)
    across = lax.broadcasted_iota(I32, (LANES, LANES), 1)
    row16 = lax.broadcasted_iota(I32, (2 * SUBS, LANES), 0)
    parts = []
    for s in range(bond_rows):
        hot_head[:, s * LANES : (s + 1) * LANES] = jnp.where(
            deep == wide(head_lane[s : s + 1], LANES), 1.0, 0.0
        ).astype(BF16)
        number = lane[0:1] + (s * LANES + 1)
        high = (number - (number & 7)).astype(F32)
        low = (number & 7).astype(F32)
        match = row16 == wide(head_tile[s : s + 1], 2 * SUBS)
        parts.append(jnp.concatenate(
            [jnp.where(match, wide(high, 16), 0.0), jnp.where(match, wide(low, 16), 0.0)], axis=0
        ).astype(BF16))
    owner_of = dot_nt(jnp.concatenate(parts, axis=1), hot_head[...])
    owner_of = owner_of[:16] + owner_of[16:]
    free = jnp.where(owner_of == 0.0, 1.0, 0.0).astype(BF16)
    before = dot_nn(free, jnp.where(deep < across, 1.0, 0.0).astype(BF16))
    totals = dot_nn(free, jnp.ones((LANES, LANES), BF16))
    for q in range(atom_rows - 1):
        before = before + jnp.where(row16 > q, wide(totals[q : q + 1], 16), 0.0)
    place_of = jnp.where(owner_of > 0.0, owner_of - 1.0, before + float(bonds)).astype(I32)
    spot = gather(place_of, tail_tile, tail_lane, 0, atom_rows)
    spot = jnp.where(is_far, -1, spot)
    spot_tile, spot_lane = lax.shift_right_arithmetic(spot, 7), spot & (LANES - 1)

    label = jnp.where(is_far, slot, -1)
    for _ in range(ORDER + 1):
        label = jnp.where(is_far, slot, gather(label, spot_tile, spot_lane, -1))
    label_tile, label_lane = lax.shift_right_arithmetic(label, 7), label & (LANES - 1)

    def columns(index, dest):
        col = index.astype(F32).T
        line = lane[0:1].astype(F32)
        for s in range(bond_rows):
            dest[s * LANES : (s + 1) * LANES, :] = jnp.where(
                col[:, s : s + 1] == line, 1.0, 0.0
            ).astype(BF16)

    columns(spot_lane, hot_tail)
    columns(label_lane, hot_root)
    for s in range(bond_rows):
        mask_tail[16 * s : 16 * s + 16, :] = jnp.where(
            row16 == wide(spot_tile[s : s + 1], 16), 1.0, 0.0
        ).astype(BF16)
        for q in range(tiles):
            base = 16 * (s * tiles + q)
            mask_root[base : base + 16, :] = jnp.where(
                wide(label_tile[s : s + 1], 16) == q, 1.0, 0.0
            ).astype(BF16)

    old_pos = old + pos0 + [mass]
    at_head = [gather(v, head_tile, head_lane) for v in old_pos]
    at_tail = [gather(v, tail_tile, tail_lane) for v in old_pos]

    def scatter(rows):
        halves = [half for row in rows for half in split(row)]
        parts = []
        for s in range(bond_rows):
            mask = mask_tail[16 * s : 16 * s + 16, :]
            parts.append(jnp.concatenate(
                [wide(half[s : s + 1], 16).astype(BF16) * mask for half in halves], axis=0
            ))
        out = dot_nn(jnp.concatenate(parts, axis=1), hot_tail[...])
        return [out[32 * i : 32 * i + 16] + out[32 * i + 16 : 32 * i + 32] for i in range(len(rows))]

    def spread(rows):
        pulls = [bent[d] * row for row in rows for d in range(3)]
        sums = scatter(pulls)
        return [
            jnp.concatenate([p - t[:bond_rows], -t[bond_rows:slot_rows]], axis=0)
            for p, t in zip(pulls, sums)
        ]

    def meet(moves):
        return [
            mass_head * m[:bond_rows] - near_mass * gather(m, spot_tile, spot_lane) for m in moves
        ]

    def bend(vector):
        return bent[0] * vector[0] + bent[1] * vector[1] + bent[2] * vector[2]

    def to_slots(rows):
        count = -(-len(rows) // SUBS)
        for v in range(count * SUBS):
            stage[SUBS * v : SUBS * v + SUBS, :] = (
                rows[v] if v < len(rows) and rows[v] is not None else jnp.zeros((SUBS, LANES), F32)
            )
        parts = []
        for s in range(bond_rows):
            value = jnp.concatenate(
                [stage[pl.ds(SUBS * SUBS * c + s, SUBS, stride=SUBS), :] for c in range(count)], axis=0
            )
            high, low = split(value)
            both = jnp.concatenate([high, low], axis=0).astype(BF16)
            size = both.shape[0]
            pieces = []
            for q in range(tiles):
                base = 16 * (s * tiles + q)
                mask = mask_root[base : base + 16, :]
                pieces.append(both * jnp.concatenate([mask] * (size // 16), axis=0))
            parts.append(jnp.concatenate(pieces, axis=0))
        out = dot_nn(jnp.concatenate(parts, axis=1), hot_root[...])
        half = SUBS * count
        return [
            [
                out[2 * half * q + SUBS * c : 2 * half * q + SUBS * c + SUBS]
                + out[2 * half * q + half + SUBS * c : 2 * half * q + half + SUBS * c + SUBS]
                for c in range(count)
            ]
            for q in range(tiles)
        ]

    def to_bonds(slots, row):
        total = jnp.zeros((bond_rows, LANES), F32)
        for q in range(tiles):
            total = jnp.where(
                label_tile == q, lanes_at(wide(slots[q][row : row + 1], bond_rows), label_lane), total
            )
        return total

    flags = jnp.where(is_far, 1.0, 0.0)
    steps = [(k, d) for k in range(ORDER + 1) for d in range(3)]
    pad = 2 * SUBS - len(steps)
    step_dims = [d for _, d in steps] + [0] * pad
    step_terms = [k for k, _ in steps] + [ORDER + 1] * pad
    quad = [(g, a, b) for g in range(ORDER) for a, b in SYM]
    dims_at = [pick_rows(step_dims[SUBS * c : SUBS * c + SUBS]) for c in range(2)]
    terms_at = [pick_rows(step_terms[SUBS * c : SUBS * c + SUBS]) for c in range(2)]
    quads_at = [
        [pick_rows([x[i] + (3 if i == 0 else 0) for x in quad[SUBS * c : SUBS * c + SUBS]]) for i in range(3)]
        for c in range(len(quad) // SUBS)
    ]

    arrive(first)
    far = [transpose8(in0[0, SUBS * q : SUBS * q + SUBS, :]) for q in range(tiles)]
    at_tail = [jnp.where(is_far, to_bonds(far, g), v) for g, v in enumerate(at_tail)]
    bond_old = [at_head[d] - at_tail[d] for d in range(3)]
    bond_new = [at_head[3 + d] - at_tail[3 + d] for d in range(3)]
    mass_head, mass_tail = at_head[6], at_tail[6]
    length = jnp.maximum(
        jnp.sqrt(bond_old[0] * bond_old[0] + bond_old[1] * bond_old[1] + bond_old[2] * bond_old[2]), 0.5
    )
    direction = [b / length for b in bond_old]
    scale = 1.0 / jnp.sqrt(mass_head + mass_tail)
    bent = [scale * d for d in direction]
    near_mass = jnp.where(is_far, 0.0, mass_tail)
    right1 = scale * (
        direction[0] * bond_new[0] + direction[1] * bond_new[1] + direction[2] * bond_new[2] - length
    )

    terms, fars = [right1], [flags]
    term_moves, term_meets, far_moves, far_meets = [], [], [], []

    def advance():
        moves = spread([terms[-1], fars[-1]])
        meets = meet(moves)
        term_moves.append(moves[:3])
        far_moves.append(moves[3:])
        term_meets.append(meets[:3])
        far_meets.append(meets[3:])
        terms.append(terms[-1] - bend(meets[:3]))
        fars.append(fars[-1] - bend(meets[3:]))

    half = ORDER // 2
    for _ in range(half):
        advance()

    def at_far(values, k):
        return fars[max(0, k - half)] * values[min(k, half)]

    slots1 = to_slots(
        [bent[d] * flags for d in range(3)] + [flags] + [at_far(fars, k) for k in range(1, ORDER)]
        + [None] + [at_far(terms, k) for k in range(ORDER + 1)]
    )
    normal = [s[0] for s in slots1]

    def send_terms(values, out):
        for q in range(tiles):
            for c in range(2):
                product = subs_at(normal[q], dims_at[c]) * subs_at(values[q], terms_at[c])
                out[c, SUBS * q : SUBS * q + SUBS, :] = transpose8(product)

    send_terms([s[1] for s in slots1], out1)
    for q in range(tiles):
        for c, (gap, a, b) in enumerate(quads_at):
            product = subs_at(normal[q], a) * subs_at(normal[q], b) * subs_at(normal[q], gap)
            out1[2 + c, SUBS * q : SUBS * q + SUBS, :] = transpose8(product)
    second = copies(1, out1, in1, forth, True, False)

    for _ in range(ORDER - half):
        advance()
    last_moves = spread([terms[ORDER]])
    last_meets = meet(last_moves)
    upper = pick_rows([0] * 4 + [1] * 4)
    normal_a = [subs_at(n, upper) for n in normal]
    normal_b = [subs_at(n, pick_rows([2] * 8)) for n in normal]
    base1 = sum(terms[1:], terms[0])

    arrive(second)

    def collect(land):
        found = []
        for part in range(land.shape[0]):
            total = land[part, 0:SUBS, :]
            for q in range(1, tiles):
                total = total + land[part, SUBS * q : SUBS * q + SUBS, :]
            for shift in (4, 2, 1):
                total = total + pltpu.roll(total, shift, 0)
            for g in range(SUBS):
                found.append(lanes_at(total, entry + width * g))
        return found

    heavy = in0[0, hub_row : hub_row + 1, :] if hub_row != centre else out0[0, 0:1, :]
    mass_send = lanes_at(wide(heavy), entry + 6 * width)
    got = collect(in1)
    matrix = [
        {ab: -mass_send * got[2 * SUBS + 6 * g + i] for i, ab in enumerate(SYM)} for g in range(ORDER)
    ]

    def owner(got, out):
        moved = []
        for k in range(ORDER + 1):
            total = [-mass_send * got[3 * k + d] for d in range(3)]
            for i in range(k):
                push = matrix[k - 1 - i]
                for d in range(3):
                    for e in range(3):
                        total[d] = total[d] + push[(min(d, e), max(d, e))] * moved[i][e]
            moved.append(total)
        for c in range(2):
            message = jnp.zeros((SUBS, LANES), F32)
            for g in range(SUBS):
                v = SUBS * c + g
                if v < 3 * ORDER:
                    value = moved[v % ORDER][v // ORDER]
                elif v < 3 * ORDER + 3:
                    value = sum([m[v - 3 * ORDER] for m in moved[1:]], moved[0][v - 3 * ORDER])
                else:
                    continue
                message = jnp.where(group == g, value, message)
            out[c] = message

    owner(got, out2)
    third = copies(2, out2, in2, back, False, True)

    weights, weight_moves, weight_meets = [], [], []
    for k in range(ORDER):
        if k == 0:
            weights.append(fars[0])
            weight_moves.append(far_moves[0])
            weight_meets.append(far_meets[0])
        else:
            weights.append(weights[-1] + fars[k])
            weight_moves.append([a + b for a, b in zip(weight_moves[-1], far_moves[k])])
            weight_meets.append([a + b for a, b in zip(weight_meets[-1], far_meets[k])])
    base_moves = [sum([m[d] for m in term_moves], last_moves[d]) for d in range(3)]
    base_meets = [sum([m[d] for m in term_meets], last_meets[d]) for d in range(3)]

    def answers(land):
        low = [transpose8(land[0, SUBS * q : SUBS * q + SUBS, :]) for q in range(tiles)]
        high = [transpose8(land[1, SUBS * q : SUBS * q + SUBS, :]) for q in range(tiles)]
        replies = []
        for q in range(tiles):
            product = low[q] * normal_a[q]
            replies.append(product + pltpu.roll(product, 4, 0) + high[q] * normal_b[q])
        return [to_bonds(replies, k) for k in range(ORDER)], high

    def through(weights, injected):
        total = weights[0] * injected[ORDER - 1]
        for k in range(1, ORDER):
            total = total + weights[k] * injected[ORDER - 1 - k]
        return total

    arrive(third)
    injected1, high = answers(in2)
    tail_moves = [to_bonds(high, 4 + d) for d in range(3)]
    sol1 = base1 + through(weights, injected1)
    stretch = [
        bond_new[d]
        - (base_meets[d] + through([w[d] for w in weight_meets], injected1) - flags * tail_moves[d])
        for d in range(3)
    ]
    current = stretch[0] * stretch[0] + stretch[1] * stretch[1] + stretch[2] * stretch[2]
    square = length * length
    goal = jnp.sqrt(jnp.maximum(2.0 * square - current, 0.5 * square))
    right2 = scale * (length - goal)
    slots3 = to_slots([fars[k] * right2 for k in range(ORDER + 1)])
    send_terms([s[0] for s in slots3], out3)
    fourth = copies(3, out3, in3, forth, True, False)

    term, both = right2, sol1 + right2
    for k in range(ORDER + 1):
        moves = spread([term])
        base_moves = [a + b for a, b in zip(base_moves, moves)]
        if k < ORDER:
            term = term - bend(meet(moves))
            both = both + term
        if k == 1:
            arrive(fourth)
            owner(collect(in3), out4)
            fifth = copies(4, out4, in4, back, False, True)

    place_tile = lax.shift_right_logical(place_of[:atom_rows], 7)
    place_lane = place_of[:atom_rows] & (LANES - 1)
    number = lax.broadcasted_iota(I32, (atom_rows, LANES), 0) * LANES + lax.broadcasted_iota(
        I32, (atom_rows, LANES), 1
    )
    entry_of = jnp.full((atom_rows, LANES), -1, I32)
    for e in range(send_count):
        entry_of = jnp.where(number == wide(send_rep[0:1, e : e + 1] + jnp.zeros((1, LANES), I32), atom_rows), e, entry_of)
    sent = entry_of >= 0
    entry_of = jnp.maximum(entry_of, 0)

    arrive(fifth)
    injected2, _ = answers(in4)
    both = both + through(weights, injected2)
    mult_ref[0, 0] = both.reshape(1, bonds)
    injected = [a + b for a, b in zip(injected1, injected2)]
    own = wide(in2[1, centre : centre + 1, :] + in4[1, centre : centre + 1, :], atom_rows)
    for d in range(3):
        total = jnp.concatenate(
            [
                base_moves[d][:bond_rows]
                + through([w[d][:bond_rows] for w in weight_moves], injected),
                base_moves[d][bond_rows:],
            ],
            axis=0,
        )
        result = pos0[d] - mass * gather(total, place_tile, place_lane)
        result = result - jnp.where(sent, lanes_at(own, entry_of + width * (4 + d)), 0.0)
        pos_ref[d, 0, 0] = result.reshape(1, atoms)
    for copy in pending:
        copy.wait_send()


def per_device(axes, sizes, old_pos, displacement, inv_mass, bond_head, bond_tail, send_list):
    atoms, bonds, send_count = old_pos.shape[-1], bond_head.shape[-1], send_list.shape[-1]
    rows = 4 * SUBS
    vmem = lambda *shape: pltpu.VMEM(shape + (LANES,), F32)
    half = lambda *shape: pltpu.VMEM(shape, BF16)
    bond_rows = bonds // LANES
    return pl.pallas_call(
        functools.partial(kernel, axes, sizes, send_count),
        out_shape=(
            jax.ShapeDtypeStruct(old_pos.shape, F32),
            jax.ShapeDtypeStruct(bond_head.shape, F32),
        ),
        in_specs=[pl.BlockSpec(memory_space=pltpu.VMEM)] * 6,
        out_specs=(pl.BlockSpec(memory_space=pltpu.VMEM), pl.BlockSpec(memory_space=pltpu.VMEM)),
        scratch_shapes=[
            vmem(atoms // LANES * SUBS),
            half(LANES, bonds), half(bonds, LANES), half(bonds, LANES),
            half(16 * bond_rows, LANES), half(16 * bond_rows * 4, LANES),
            vmem(2 * SUBS * SUBS),
            vmem(1, SUBS), vmem(1, rows),
            vmem(5, rows), vmem(5, rows),
            vmem(2, SUBS), vmem(2, rows),
            vmem(2, rows), vmem(2, rows),
            vmem(2, SUBS), vmem(2, rows),
            pltpu.SemaphoreType.DMA((5, 27)),
            pltpu.SemaphoreType.DMA((5, 27)),
        ],
        compiler_params=pltpu.CompilerParams(
            collective_id=0, has_side_effects=True, vmem_limit_bytes=56 * 1024 * 1024
        ),
    )(old_pos, displacement, inv_mass, bond_head, bond_tail, send_list)


def solution(mesh):
    axes = ("gx", "gy", "gz")
    sizes = tuple(mesh.shape[name] for name in axes)
    return jax.shard_map(
        functools.partial(per_device, axes, sizes),
        mesh=mesh,
        in_specs=(
            P(None, "gx", "gy", "gz", None),
            P(None, "gx", "gy", "gz", None),
            P("gx", "gy", "gz", None),
            P("gx", "gy", "gz", None),
            P("gx", "gy", "gz", None),
            P("gx", "gy", "gz", None),
        ),
        out_specs=(P(None, "gx", "gy", "gz", None), P("gx", "gy", "gz", None)),
        check_vma=False,
    )
```

time: 50.7 us -> 34.9 us (0.69)
  Pallas kernels: 47.9 us -> 32.1 us
    pallas_call x1, Pallas kernels: 47.9 us -> 32.1 us  [per_device(): pl.pallas_call(functools.partial(kernel, axes, sizes, send_count), out_sh...]
where the time goes in v1:
time: 34.9 us; the launch traced here: 34.6 us
  Pallas kernels  32.1 us (92%)
  local copies, waits for them, and re-layouts  1.93 us (6%)
  between operations  0.65 us (2%)
    pallas_call x1, Pallas kernels, per_device(): pl.pallas_call(functools.partial(kernel, axes, sizes, send_count), out_sh...  32.1 us
    unnamed x4, local copies, waits for them, and re-layouts  1.93 us

profile of v1, /device:TPU:0, one launch (start us, length us, event | category | flops | bytes accessed | tf_op | source)
XLA Modules:
  0.0 34.6 jit_solution(5291435636688621570)
XLA Ops:
  0.6 32.1 %shard_map.77 = (f32[3,1,1,1,1536]{4,3,2,1,0:T(1,128)}, f32[1,1,1,1024]{3,2,1,0:T(1,128)}) custom-call(f32[3,1,1,1,1536]{4,3,2,1,0:T(1,128)} %old_ref.1, f32[3,1,1,1,1536]{4,3,2,1,0:T(1,128)} %move_ref.1, f32[1,1,1,1536]{3,2,1,0:T(1,128)} %mass_ref.1, s32[1,1,1,1024]{3,2,1,0:T(1,128)} %head_ref.1, s32[1,1,1,1024]{3,2,1,0:T(1,128)} %tail_ref.1, ...), custom_call_target="tpu_custom_call" | custom-call | tf_op jit(solution)/shard_map/pallas_call | solution.py:536
  32.7 0.0 copy-start
  32.7 1.3 %copy.10 = f32[3,1,1,1,1536]{4,3,2,1,0:T(1,128)} copy(f32[3,1,1,1,1536]{4,3,2,1,0:T(1,128)} %get-tuple-element.4) | data formatting | bytes 36864
  34.1 0.0 copy-done
  34.1 0.6 %copy.11 = f32[1,1,1,1024]{3,2,1,0:T(1,128)} copy(f32[1,1,1,1024]{3,2,1,0:T(1,128)S(1)} %copy-done) | data formatting | bytes 8192
Async XLA Ops:
  32.7 1.3 %copy-start = (f32[1,1,1,1024]{3,2,1,0:T(1,128)S(1)}, f32[1,1,1,1024]{3,2,1,0:T(1,128)}, u32[]{:S(2)}) copy-start(f32[1,1,1,1024]{3,2,1,0:T(1,128)} %get-tuple-element.5) | copy-start | bytes 12292

commit v2 on v1

--- a/solution.py
+++ b/solution.py
@@ -45,7 +45,9 @@
 
 
 def routes(sizes):
-    classes = [(a, b, c) for a in range(3) for b in range(3) for c in range(3)]
+    plane = [(a, c) for a in range(3) for c in range(3)]
+    classes = [(a, b, c) for b in (0, 2, 1) for a, c in plane[:SUBS]]
+    classes += [plane[SUBS][:1] + (b,) + plane[SUBS][1:] for b in (0, 2, 1)]
     direct, forth, back = [], [], []
     for cls in classes:
         direct.append(tuple((1 - c) for c in cls))
@@ -56,8 +58,9 @@
 
 def kernel(
     axes, sizes, send_count,
-    old_ref, move_ref, mass_ref, head_ref, tail_ref, send_ref,
+    old_hbm, move_hbm, mass_hbm, head_hbm, tail_hbm, send_hbm,
     pos_ref, mult_ref,
+    old_ref, move_ref, mass_ref, head_ref, tail_ref, send_ref, load_sem,
     table, hot_head, hot_tail, hot_root, mask_tail, mask_root, stage,
     out0, in0, out1, in1, out2, in2, out3, in3, out4, in4,
     send_sem, recv_sem,
@@ -74,6 +77,8 @@
     here = [lax.axis_index(name) for name in axes]
     turn = [1 - 2 * lax.rem(i, 2) if flips(n) else 1 for i, n in zip(here, sizes)]
 
+    twin = sizes[1] == 2
+
     def nowhere(offset):
         return all(o % n == 0 for o, n in zip(offset, sizes))
 
@@ -88,6 +93,15 @@
             key = tuple(o % n for o, n in zip(offset, sizes))
             if any(key) and key not in [k for k, _ in greet]:
                 greet.append((key, offset))
+    loads = [
+        pltpu.make_async_copy(source, dest, load_sem.at[i])
+        for i, (source, dest) in enumerate((
+            (send_hbm, send_ref), (old_hbm, old_ref), (move_hbm, move_ref), (mass_hbm, mass_ref),
+            (head_hbm, head_ref), (tail_hbm, tail_ref),
+        ))
+    ]
+    for load in loads:
+        load.start()
     barrier = pltpu.get_barrier_semaphore()
     for _, offset in greet:
         pl.semaphore_signal(barrier, inc=1, device_id=target(offset), device_id_type=MESH)
@@ -103,12 +117,8 @@
         x = pltpu.roll(x, 0, 1, stride=width, stride_axis=0)
         return lanes_at(subs_at(x, swap), unskew)
 
-    def pick_rows(choice):
-        index = jnp.zeros((SUBS, LANES), I32)
-        for j, c in enumerate(choice):
-            if c:
-                index = jnp.where(sub == j, c, index)
-        return index
+    for load in loads:
+        load.wait()
 
     old = [old_ref[k, 0, 0].reshape(atom_rows, LANES) for k in range(3)]
     pos0 = [old[k] + move_ref[k, 0, 0].reshape(atom_rows, LANES) for k in range(3)]
@@ -133,38 +143,8 @@
         for part in range(land.shape[0]):
             land[part, centre : centre + 1, :] = jnp.zeros((1, LANES), F32)
             land[part, len(classes) :, :] = jnp.zeros((SUBS * tiles - len(classes), LANES), F32)
-
-    pl.semaphore_wait(barrier, len(greet))
-
-    order = sorted(range(len(classes)), key=lambda r: -(classes[r][0] + classes[r][2]))
-
-    def copies(step, source, landing, offsets, each, whole):
-        started = []
-        for row in order:
-            if row == centre and not whole:
-                continue
-            line = row if each else 0
-            if nowhere(offsets[row]):
-                landing[:, row : row + 1, :] = source[:, line : line + 1, :]
-                continue
-            copy = pltpu.make_async_remote_copy(
-                source.at[:, line], landing.at[:, row],
-                send_sem.at[step, row], recv_sem.at[step, row],
-                device_id=target(offsets[row]), device_id_type=MESH,
-            )
-            copy.start()
-            started.append(copy)
-        return started
-
-    pending = []
-
-    def arrive(started):
-        for copy in started:
-            copy.wait_recv()
-        pending.extend(started)
-
-    first = copies(0, out0, in0, direct, False, False)
-
+            if twin:
+                land[part, 3 * SUBS + 1 : 3 * SUBS + 2, :] = jnp.zeros((1, LANES), F32)
     head = head_ref[0, 0].reshape(bond_rows, LANES)
     tail = tail_ref[0, 0].reshape(bond_rows, LANES)
     head_tile, head_lane = lax.shift_right_logical(head, 7), head & (LANES - 1)
@@ -181,7 +161,10 @@
         1 - s * (b - 1) if flips(n) else b
         for b, s, n in zip((bx, by, bz), turn, sizes)
     ]
-    slot = ((place[0] * 3 + place[1]) * 3 + place[2]) * width + (slot & (width - 1))
+    across_plane = place[0] * 3 + place[2]
+    level = jnp.where(place[1] == 0, 0, 3 - place[1])
+    slot_row = jnp.where(across_plane < SUBS, SUBS * level + across_plane, 3 * SUBS + level)
+    slot = slot_row * width + (slot & (width - 1))
 
     def gather(rows, tile, index, start=0.0, count=None):
         shape = index.shape
@@ -257,20 +240,20 @@
         out = dot_nn(jnp.concatenate(parts, axis=1), hot_tail[...])
         return [out[32 * i : 32 * i + 16] + out[32 * i + 16 : 32 * i + 32] for i in range(len(rows))]
 
-    def spread(rows):
+    def spread(bent, rows):
         pulls = [bent[d] * row for row in rows for d in range(3)]
         sums = scatter(pulls)
         return [
             jnp.concatenate([p - t[:bond_rows], -t[bond_rows:slot_rows]], axis=0)
             for p, t in zip(pulls, sums)
-        ]
+        ], sums
 
     def meet(moves):
         return [
             mass_head * m[:bond_rows] - near_mass * gather(m, spot_tile, spot_lane) for m in moves
         ]
 
-    def bend(vector):
+    def bend(bent, vector):
         return bent[0] * vector[0] + bent[1] * vector[1] + bent[2] * vector[2]
 
     def to_slots(rows):
@@ -313,81 +296,195 @@
         return total
 
     flags = jnp.where(is_far, 1.0, 0.0)
-    steps = [(k, d) for k in range(ORDER + 1) for d in range(3)]
-    pad = 2 * SUBS - len(steps)
-    step_dims = [d for _, d in steps] + [0] * pad
-    step_terms = [k for k, _ in steps] + [ORDER + 1] * pad
-    quad = [(g, a, b) for g in range(ORDER) for a, b in SYM]
-    dims_at = [pick_rows(step_dims[SUBS * c : SUBS * c + SUBS]) for c in range(2)]
-    terms_at = [pick_rows(step_terms[SUBS * c : SUBS * c + SUBS]) for c in range(2)]
-    quads_at = [
-        [pick_rows([x[i] + (3 if i == 0 else 0) for x in quad[SUBS * c : SUBS * c + SUBS]]) for i in range(3)]
-        for c in range(len(quad) // SUBS)
-    ]
+    slot_tile, slot_lane = lax.shift_right_logical(slot, 7), slot & (LANES - 1)
+    parts = []
+    for s in range(bond_rows):
+        number = lane[0:1] + (s * LANES + 1)
+        high = (number - (number & 7)).astype(F32)
+        low = (number & 7).astype(F32)
+        match = jnp.where(is_far[s : s + 1], slot_tile[s : s + 1], -1)
+        match = row16 == wide(match, 2 * SUBS)
+        parts.append(jnp.concatenate(
+            [jnp.where(match, wide(high, 16), 0.0), jnp.where(match, wide(low, 16), 0.0)], axis=0
+        ).astype(BF16))
+    bond_of = dot_nn(jnp.concatenate(parts, axis=1), hot_root[...])
+    bond_of = (bond_of[:SUBS] + bond_of[16 : 16 + SUBS]).astype(I32) - 1
+    bond_tile, bond_lane = lax.shift_right_arithmetic(bond_of, 7), bond_of & (LANES - 1)
+
+
+    order = sorted(range(len(classes)), key=lambda r: -(classes[r][0] + classes[r][2]))
+
+    def copies(step, source, landing, offsets, each, whole):
+        started = []
+        for row in order:
+            if row == centre and not whole or twin and classes[row][1] == 2:
+                continue
+            line = row if each else 0
+            if nowhere(offsets[row]):
+                landing[:, row : row + 1, :] = source[:, line : line + 1, :]
+                continue
+            copy = pltpu.make_async_remote_copy(
+                source.at[:, line], landing.at[:, row],
+                send_sem.at[step, row], recv_sem.at[step, row],
+                device_id=target(offsets[row]), device_id_type=MESH,
+            )
+            copy.start()
+            started.append(copy)
+        return started
+
+    def post(out, part, value):
+        pieces = [value[SUBS * q : SUBS * q + SUBS] for q in range(tiles)]
+        if twin:
+            pieces[0] = pieces[0] + pieces[1]
+            pieces[3] = pieces[3] + jnp.where(sub == 0, wide(pieces[3][1:2]), 0.0)
+        for q in range(tiles):
+            if not (twin and q == 1):
+                out[part, SUBS * q : SUBS * q + SUBS, :] = pieces[q]
+
+    def landed(land, part):
+        parts = [land[part, SUBS * q : SUBS * q + SUBS, :] for q in range(tiles)]
+        if twin:
+            parts[1] = parts[0]
+            parts[3] = jnp.where(sub == 1, wide(parts[3][0:1]), parts[3])
+        return parts
+
+    pending = []
+
+    def arrive(started):
+        for copy in started:
+            copy.wait_recv()
+        pending.extend(started)
+
+    pl.semaphore_wait(barrier, len(greet))
+    first = copies(0, out0, in0, direct, False, False)
+
+    mass_head = at_head[6]
+
+    def geometry(head_data, tail_data):
+        olds = [head_data[d] - tail_data[d] for d in range(3)]
+        news = [head_data[3 + d] - tail_data[3 + d] for d in range(3)]
+        size = jnp.maximum(jnp.sqrt(olds[0] * olds[0] + olds[1] * olds[1] + olds[2] * olds[2]), 0.5)
+        direction = [b / size for b in olds]
+        scale = 1.0 / jnp.sqrt(head_data[6] + tail_data[6])
+        right = scale * (
+            direction[0] * news[0] + direction[1] * news[1] + direction[2] * news[2] - size
+        )
+        return news, size, scale, [scale * d for d in direction], right
+
+    _, _, _, bent, right = geometry(at_head, at_tail)
+    bent = [jnp.where(is_far, 0.0, b) for b in bent]
+    near_mass = jnp.where(is_far, 0.0, at_tail[6])
+    kids = gather(flags, spot_tile, spot_lane) * near_mass
+    series = [jnp.where(is_far, 0.0, right)] + [kids * b for b in bent]
+    drive, square_of = [], []
+    for k in range(ORDER):
+        if k == ORDER - 1:
+            series = series[:1]
+        moves, sums = spread(bent, series)
+        drive.append([mass_head * sums[d][:bond_rows] * flags for d in range(3)])
+        if k < ORDER - 1:
+            square_of.append(
+                [mass_head * sums[3 + 3 * b + a][:bond_rows] * flags for a, b in SYM]
+            )
+            if k == ORDER - 2:
+                series, moves = series[:1], moves[:3]
+            meets = meet(moves)
+            series = [
+                v - bend(bent, meets[3 * i : 3 * i + 3]) for i, v in enumerate(series)
+            ]
+
+    spread_lane = width * sub + entry
+
+    def to_rows(packed, row):
+        return jnp.concatenate(
+            [lanes_at(wide(packed[q][row : row + 1]), spread_lane) for q in range(tiles)], axis=0
+        )
+
+    def from_bonds(value):
+        rows = gather(value, bond_tile, bond_lane)
+        return to_rows([rows[q : q + 1] for q in range(tiles)], 0)
+
+    used = from_bonds(jnp.ones((bond_rows, LANES), F32)) > 0.0
+    head_rows = [from_bonds(v) for v in at_head]
+    flat = [v for group in drive + square_of for v in group]
+    flat = to_slots(flat)
+    flat = [
+        to_rows([part[v // SUBS] for part in flat], v % SUBS) for v in range(3 * ORDER + 6 * (ORDER - 1))
+    ]
+    drive = [flat[3 * k : 3 * k + 3] for k in range(ORDER)]
+    square_of = [flat[3 * ORDER + 6 * k : 3 * ORDER + 6 * k + 6] for k in range(ORDER - 1)]
+    entry_rows = jnp.concatenate([entry] * tiles, axis=0)
+    group_rows = jnp.concatenate([group] * tiles, axis=0)
 
     arrive(first)
-    far = [transpose8(in0[0, SUBS * q : SUBS * q + SUBS, :]) for q in range(tiles)]
+    landing = jnp.concatenate(landed(in0, 0), axis=0)
+    tail_rows = [lanes_at(landing, entry_rows + width * g) for g in range(7)]
+    _, _, _, normal, start = geometry(head_rows, tail_rows)
+    normal = [jnp.where(used, b, 0.0) for b in normal]
+    pairs = [normal[a] * normal[b] for a, b in SYM]
+    keep = 1.0 - head_rows[6] * (pairs[0] + pairs[3] + pairs[5])
+    pushes = [
+        q[0] * pairs[0] + q[3] * pairs[3] + q[5] * pairs[5]
+        + 2.0 * (q[1] * pairs[1] + q[2] * pairs[2] + q[4] * pairs[4])
+        for q in square_of
+    ]
+    chain, reply = [start], [None, keep]
+    for k in range(1, ORDER + 1):
+        value = keep * chain[-1] + (
+            normal[0] * drive[k - 1][0] + normal[1] * drive[k - 1][1] + normal[2] * drive[k - 1][2]
+        )
+        for i in range(k - 1):
+            value = value + pushes[k - 2 - i] * chain[i]
+        chain.append(value)
+    for k in range(2, ORDER):
+        value = keep * reply[-1] + pushes[k - 2]
+        for i in range(1, k - 1):
+            value = value + pushes[k - 2 - i] * reply[i]
+        reply.append(value)
+
+    def packed(values):
+        total = jnp.zeros((SUBS * tiles, LANES), F32)
+        for g, value in enumerate(values):
+            total = jnp.where(group_rows == g, value, total)
+        return total
+
+    def post_terms(values, out):
+        steps = [normal[d] * values[k] for k in range(ORDER + 1) for d in range(3)]
+        post(out, 0, packed(steps[:SUBS]))
+        post(out, 1, packed(steps[SUBS:]))
+
+    post_terms(chain, out1)
+    quads = [p if reply[g] is None else reply[g] * p for g in range(ORDER) for p in pairs]
+    for c in range(len(quads) // SUBS):
+        post(out1, 2 + c, packed(quads[SUBS * c : SUBS * c + SUBS]))
+    second = copies(1, out1, in1, forth, True, False)
+
+    low = packed([normal[0]] * 4 + [normal[1]] * 4)
+    normal_a = [transpose8(low[SUBS * q : SUBS * q + SUBS]) for q in range(tiles)]
+    normal_b = [
+        transpose8(normal[2][SUBS * q : SUBS * q + SUBS]) for q in range(tiles)
+    ]
+    far = [transpose8(piece) for piece in landed(in0, 0)]
     at_tail = [jnp.where(is_far, to_bonds(far, g), v) for g, v in enumerate(at_tail)]
-    bond_old = [at_head[d] - at_tail[d] for d in range(3)]
-    bond_new = [at_head[3 + d] - at_tail[3 + d] for d in range(3)]
-    mass_head, mass_tail = at_head[6], at_tail[6]
-    length = jnp.maximum(
-        jnp.sqrt(bond_old[0] * bond_old[0] + bond_old[1] * bond_old[1] + bond_old[2] * bond_old[2]), 0.5
-    )
-    direction = [b / length for b in bond_old]
-    scale = 1.0 / jnp.sqrt(mass_head + mass_tail)
-    bent = [scale * d for d in direction]
-    near_mass = jnp.where(is_far, 0.0, mass_tail)
-    right1 = scale * (
-        direction[0] * bond_new[0] + direction[1] * bond_new[1] + direction[2] * bond_new[2] - length
-    )
+    bond_new, length, scale, bent, right1 = geometry(at_head, at_tail)
 
     terms, fars = [right1], [flags]
     term_moves, term_meets, far_moves, far_meets = [], [], [], []
 
     def advance():
-        moves = spread([terms[-1], fars[-1]])
+        moves, _ = spread(bent, [terms[-1], fars[-1]])
         meets = meet(moves)
         term_moves.append(moves[:3])
         far_moves.append(moves[3:])
         term_meets.append(meets[:3])
         far_meets.append(meets[3:])
-        terms.append(terms[-1] - bend(meets[:3]))
-        fars.append(fars[-1] - bend(meets[3:]))
-
-    half = ORDER // 2
-    for _ in range(half):
+        terms.append(terms[-1] - bend(bent, meets[:3]))
+        fars.append(fars[-1] - bend(bent, meets[3:]))
+
+    for _ in range(ORDER):
         advance()
-
-    def at_far(values, k):
-        return fars[max(0, k - half)] * values[min(k, half)]
-
-    slots1 = to_slots(
-        [bent[d] * flags for d in range(3)] + [flags] + [at_far(fars, k) for k in range(1, ORDER)]
-        + [None] + [at_far(terms, k) for k in range(ORDER + 1)]
-    )
-    normal = [s[0] for s in slots1]
-
-    def send_terms(values, out):
-        for q in range(tiles):
-            for c in range(2):
-                product = subs_at(normal[q], dims_at[c]) * subs_at(values[q], terms_at[c])
-                out[c, SUBS * q : SUBS * q + SUBS, :] = transpose8(product)
-
-    send_terms([s[1] for s in slots1], out1)
-    for q in range(tiles):
-        for c, (gap, a, b) in enumerate(quads_at):
-            product = subs_at(normal[q], a) * subs_at(normal[q], b) * subs_at(normal[q], gap)
-            out1[2 + c, SUBS * q : SUBS * q + SUBS, :] = transpose8(product)
-    second = copies(1, out1, in1, forth, True, False)
-
-    for _ in range(ORDER - half):
-        advance()
-    last_moves = spread([terms[ORDER]])
+    last_moves, _ = spread(bent, [terms[ORDER]])
     last_meets = meet(last_moves)
-    upper = pick_rows([0] * 4 + [1] * 4)
-    normal_a = [subs_at(n, upper) for n in normal]
-    normal_b = [subs_at(n, pick_rows([2] * 8)) for n in normal]
     base1 = sum(terms[1:], terms[0])
 
     arrive(second)
@@ -397,7 +494,8 @@
         for part in range(land.shape[0]):
             total = land[part, 0:SUBS, :]
             for q in range(1, tiles):
-                total = total + land[part, SUBS * q : SUBS * q + SUBS, :]
+                if not (twin and q == 1):
+                    total = total + land[part, SUBS * q : SUBS * q + SUBS, :]
             for shift in (4, 2, 1):
                 total = total + pltpu.roll(total, shift, 0)
             for g in range(SUBS):
@@ -451,13 +549,13 @@
     base_meets = [sum([m[d] for m in term_meets], last_meets[d]) for d in range(3)]
 
     def answers(land):
-        low = [transpose8(land[0, SUBS * q : SUBS * q + SUBS, :]) for q in range(tiles)]
-        high = [transpose8(land[1, SUBS * q : SUBS * q + SUBS, :]) for q in range(tiles)]
+        low = [transpose8(piece) for piece in landed(land, 0)]
+        high = [transpose8(piece) for piece in landed(land, 1)]
         replies = []
         for q in range(tiles):
             product = low[q] * normal_a[q]
             replies.append(product + pltpu.roll(product, 4, 0) + high[q] * normal_b[q])
-        return [to_bonds(replies, k) for k in range(ORDER)], high
+        return replies, high
 
     def through(weights, injected):
         total = weights[0] * injected[ORDER - 1]
@@ -466,7 +564,8 @@
         return total
 
     arrive(third)
-    injected1, high = answers(in2)
+    replies1, high = answers(in2)
+    injected1 = [to_bonds(replies1, k) for k in range(ORDER)]
     tail_moves = [to_bonds(high, 4 + d) for d in range(3)]
     sol1 = base1 + through(weights, injected1)
     stretch = [
@@ -479,15 +578,16 @@
     goal = jnp.sqrt(jnp.maximum(2.0 * square - current, 0.5 * square))
     right2 = scale * (length - goal)
     slots3 = to_slots([fars[k] * right2 for k in range(ORDER + 1)])
-    send_terms([s[0] for s in slots3], out3)
+    slots3 = [part[0] for part in slots3]
+    post_terms([to_rows(slots3, k) for k in range(ORDER + 1)], out3)
     fourth = copies(3, out3, in3, forth, True, False)
 
     term, both = right2, sol1 + right2
     for k in range(ORDER + 1):
-        moves = spread([term])
+        moves, _ = spread(bent, [term])
         base_moves = [a + b for a, b in zip(base_moves, moves)]
         if k < ORDER:
-            term = term - bend(meet(moves))
+            term = term - bend(bent, meet(moves))
             both = both + term
         if k == 1:
             arrive(fourth)
@@ -505,25 +605,38 @@
     sent = entry_of >= 0
     entry_of = jnp.maximum(entry_of, 0)
 
+    atom_label = jnp.where(
+        place_tile < bond_rows, gather(label, place_tile, place_lane, -1, bond_rows), -1
+    )
+    atom_tile, atom_lane = lax.shift_right_arithmetic(atom_label, 7), atom_label & (LANES - 1)
+    at_atoms = [pos0[d] - mass * gather(base_moves[d], place_tile, place_lane) for d in range(3)]
+    weight_moves = [
+        [mass * gather(w[d][:bond_rows], place_tile, place_lane) for d in range(3)]
+        for w in weight_moves
+    ]
+    early = len(pending)
+    for copy in pending:
+        copy.wait_send()
+
     arrive(fifth)
-    injected2, _ = answers(in4)
-    both = both + through(weights, injected2)
+    replies2, _ = answers(in4)
+    both = both + through(weights, [to_bonds(replies2, k) for k in range(ORDER)])
     mult_ref[0, 0] = both.reshape(1, bonds)
-    injected = [a + b for a, b in zip(injected1, injected2)]
+    replies = [a + b for a, b in zip(replies1, replies2)]
+    injected = []
+    for k in range(ORDER):
+        total = jnp.zeros((atom_rows, LANES), F32)
+        for q in range(tiles):
+            total = jnp.where(
+                atom_tile == q, lanes_at(wide(replies[q][k : k + 1], atom_rows), atom_lane), total
+            )
+        injected.append(total)
     own = wide(in2[1, centre : centre + 1, :] + in4[1, centre : centre + 1, :], atom_rows)
     for d in range(3):
-        total = jnp.concatenate(
-            [
-                base_moves[d][:bond_rows]
-                + through([w[d][:bond_rows] for w in weight_moves], injected),
-                base_moves[d][bond_rows:],
-            ],
-            axis=0,
-        )
-        result = pos0[d] - mass * gather(total, place_tile, place_lane)
+        result = at_atoms[d] - through([w[d] for w in weight_moves], injected)
         result = result - jnp.where(sent, lanes_at(own, entry_of + width * (4 + d)), 0.0)
         pos_ref[d, 0, 0] = result.reshape(1, atoms)
-    for copy in pending:
+    for copy in pending[early:]:
         copy.wait_send()
 
 
@@ -536,16 +649,20 @@
     return pl.pallas_call(
         functools.partial(kernel, axes, sizes, send_count),
         out_shape=(
-            jax.ShapeDtypeStruct(old_pos.shape, F32),
-            jax.ShapeDtypeStruct(bond_head.shape, F32),
+            pltpu.VMEM(old_pos.shape, F32),
+            pltpu.VMEM(bond_head.shape, F32),
         ),
-        in_specs=[pl.BlockSpec(memory_space=pltpu.VMEM)] * 6,
+        in_specs=[pl.BlockSpec(memory_space=pltpu.HBM)] * 6,
         out_specs=(pl.BlockSpec(memory_space=pltpu.VMEM), pl.BlockSpec(memory_space=pltpu.VMEM)),
         scratch_shapes=[
+            pltpu.VMEM(old_pos.shape, F32), pltpu.VMEM(displacement.shape, F32),
+            pltpu.VMEM(inv_mass.shape, F32), pltpu.VMEM(bond_head.shape, I32),
+            pltpu.VMEM(bond_tail.shape, I32), pltpu.VMEM(send_list.shape, I32),
+            pltpu.SemaphoreType.DMA((6,)),
             vmem(atoms // LANES * SUBS),
             half(LANES, bonds), half(bonds, LANES), half(bonds, LANES),
             half(16 * bond_rows, LANES), half(16 * bond_rows * 4, LANES),
-            vmem(2 * SUBS * SUBS),
+            vmem(4 * SUBS * SUBS),
             vmem(1, SUBS), vmem(1, rows),
             vmem(5, rows), vmem(5, rows),
             vmem(2, SUBS), vmem(2, rows),

time: 34.9 us -> 31.2 us (0.89)
  Pallas kernels: 32.1 us -> 29.2 us
  local copies, waits for them, and re-layouts: 1.93 us -> 1.2 us
    pallas_call x1, Pallas kernels: 32.1 us -> 29.2 us  [per_device(): pl.pallas_call(functools.partial(kernel, axes, sizes, send_count), out_sh...]
    unnamed x4 -> x2, local copies, waits for them, and re-layouts: 1.93 us -> 1.2 us
where the time goes in v2:
time: 31.2 us; the launch traced here: 31 us
  Pallas kernels  29.2 us (94%)
  local copies, waits for them, and re-layouts  1.2 us (4%)
  between operations  0.64 us (2%)
    pallas_call x1, Pallas kernels, per_device(): pl.pallas_call(functools.partial(kernel, axes, sizes, send_count), out_sh...  29.2 us
    unnamed x2, local copies, waits for them, and re-layouts  1.2 us

profile of v2, /device:TPU:0, one launch (start us, length us, event | category | flops | bytes accessed | tf_op | source)
XLA Modules:
  0.0 31.0 jit_solution(15828233967459058069)
XLA Ops:
  0.6 29.2 %shard_map.77 = (f32[3,1,1,1,1536]{4,3,2,1,0:T(1,128)S(1)}, f32[1,1,1,1024]{3,2,1,0:T(1,128)S(1)}) custom-call(f32[3,1,1,1,1536]{4,3,2,1,0:T(1,128)} %old_hbm.1, f32[3,1,1,1,1536]{4,3,2,1,0:T(1,128)} %move_hbm.1, f32[1,1,1,1536]{3,2,1,0:T(1,128)} %mass_hbm.1, s32[1,1,1,1024]{3,2,1,0:T(1,128)} %head_hbm.1, s32[1,1,1,1024]{3,2,1,0:T(1,128)} %tail_hbm.1, ...), custom_call_target="tpu_custom_call" | custom-call | tf_op jit(solution)/shard_map/pallas_call | solution.py:649
  29.8 0.6 %copy.10 = f32[3,1,1,1,1536]{4,3,2,1,0:T(1,128)} copy(f32[3,1,1,1,1536]{4,3,2,1,0:T(1,128)S(1)} %get-tuple-element.2) | data formatting | bytes 36864
  30.4 0.6 %copy.11 = f32[1,1,1,1024]{3,2,1,0:T(1,128)} copy(f32[1,1,1,1024]{3,2,1,0:T(1,128)S(1)} %get-tuple-element.3) | data formatting | bytes 8192

commit v3 on v2

--- a/solution.py
+++ b/solution.py
@@ -35,9 +35,13 @@
     return jnp.take_along_axis(rows, index, axis=0, mode="promise_in_bounds")
 
 
-def split(value):
-    high = value.astype(BF16).astype(F32)
-    return high, value - high
+def split(value, count=2):
+    parts = []
+    for _ in range(count - 1):
+        high = value.astype(BF16).astype(F32)
+        parts.append(high)
+        value = value - high
+    return parts + [value]
 
 
 def flips(n):
@@ -143,7 +147,7 @@
         for part in range(land.shape[0]):
             land[part, centre : centre + 1, :] = jnp.zeros((1, LANES), F32)
             land[part, len(classes) :, :] = jnp.zeros((SUBS * tiles - len(classes), LANES), F32)
-            if twin:
+            if twin and land is in3:
                 land[part, 3 * SUBS + 1 : 3 * SUBS + 2, :] = jnp.zeros((1, LANES), F32)
     head = head_ref[0, 0].reshape(bond_rows, LANES)
     tail = tail_ref[0, 0].reshape(bond_rows, LANES)
@@ -256,36 +260,40 @@
     def bend(bent, vector):
         return bent[0] * vector[0] + bent[1] * vector[1] + bent[2] * vector[2]
 
-    def to_slots(rows):
+    def to_slots(rows, pieces=2):
         count = -(-len(rows) // SUBS)
-        for v in range(count * SUBS):
+        half = SUBS * count
+        pad = pieces * count % 2
+        for v in range(half):
             stage[SUBS * v : SUBS * v + SUBS, :] = (
-                rows[v] if v < len(rows) and rows[v] is not None else jnp.zeros((SUBS, LANES), F32)
+                rows[v] if v < len(rows) else jnp.zeros((SUBS, LANES), F32)
             )
         parts = []
         for s in range(bond_rows):
             value = jnp.concatenate(
                 [stage[pl.ds(SUBS * SUBS * c + s, SUBS, stride=SUBS), :] for c in range(count)], axis=0
             )
-            high, low = split(value)
-            both = jnp.concatenate([high, low], axis=0).astype(BF16)
+            layers = split(value, pieces) + [jnp.zeros((SUBS, LANES), F32)] * pad
+            both = jnp.concatenate(layers, axis=0).astype(BF16)
             size = both.shape[0]
-            pieces = []
+            chunks = []
             for q in range(tiles):
                 base = 16 * (s * tiles + q)
                 mask = mask_root[base : base + 16, :]
-                pieces.append(both * jnp.concatenate([mask] * (size // 16), axis=0))
-            parts.append(jnp.concatenate(pieces, axis=0))
+                chunks.append(both * jnp.concatenate([mask] * (size // 16), axis=0))
+            parts.append(jnp.concatenate(chunks, axis=0))
         out = dot_nn(jnp.concatenate(parts, axis=1), hot_root[...])
-        half = SUBS * count
-        return [
-            [
-                out[2 * half * q + SUBS * c : 2 * half * q + SUBS * c + SUBS]
-                + out[2 * half * q + half + SUBS * c : 2 * half * q + half + SUBS * c + SUBS]
-                for c in range(count)
-            ]
-            for q in range(tiles)
-        ]
+        result = []
+        for q in range(tiles):
+            found = []
+            for c in range(count):
+                base = size * q + SUBS * c
+                found.append(sum(
+                    [out[base + half * p : base + half * p + SUBS] for p in range(1, pieces)],
+                    out[base : base + SUBS],
+                ))
+            result.append(found)
+        return result
 
     def to_bonds(slots, row):
         total = jnp.zeros((bond_rows, LANES), F32)
@@ -296,28 +304,12 @@
         return total
 
     flags = jnp.where(is_far, 1.0, 0.0)
-    slot_tile, slot_lane = lax.shift_right_logical(slot, 7), slot & (LANES - 1)
-    parts = []
-    for s in range(bond_rows):
-        number = lane[0:1] + (s * LANES + 1)
-        high = (number - (number & 7)).astype(F32)
-        low = (number & 7).astype(F32)
-        match = jnp.where(is_far[s : s + 1], slot_tile[s : s + 1], -1)
-        match = row16 == wide(match, 2 * SUBS)
-        parts.append(jnp.concatenate(
-            [jnp.where(match, wide(high, 16), 0.0), jnp.where(match, wide(low, 16), 0.0)], axis=0
-        ).astype(BF16))
-    bond_of = dot_nn(jnp.concatenate(parts, axis=1), hot_root[...])
-    bond_of = (bond_of[:SUBS] + bond_of[16 : 16 + SUBS]).astype(I32) - 1
-    bond_tile, bond_lane = lax.shift_right_arithmetic(bond_of, 7), bond_of & (LANES - 1)
-
-
     order = sorted(range(len(classes)), key=lambda r: -(classes[r][0] + classes[r][2]))
 
-    def copies(step, source, landing, offsets, each, whole):
-        started = []
-        for row in order:
-            if row == centre and not whole or twin and classes[row][1] == 2:
+    def copies(step, source, landing, offsets, each, whole, merge=True, only=None):
+        started = {}
+        for row in only or order:
+            if row == centre and not whole or merge and twin and classes[row][1] == 2:
                 continue
             line = row if each else 0
             if nowhere(offsets[row]):
@@ -329,7 +321,7 @@
                 device_id=target(offsets[row]), device_id_type=MESH,
             )
             copy.start()
-            started.append(copy)
+            started[row] = copy
         return started
 
     def post(out, part, value):
@@ -353,10 +345,8 @@
     def arrive(started):
         for copy in started:
             copy.wait_recv()
-        pending.extend(started)
-
-    pl.semaphore_wait(barrier, len(greet))
-    first = copies(0, out0, in0, direct, False, False)
+            pending.append(copy)
+
 
     mass_head = at_head[6]
 
@@ -376,22 +366,22 @@
     near_mass = jnp.where(is_far, 0.0, at_tail[6])
     kids = gather(flags, spot_tile, spot_lane) * near_mass
     series = [jnp.where(is_far, 0.0, right)] + [kids * b for b in bent]
-    drive, square_of = [], []
-    for k in range(ORDER):
-        if k == ORDER - 1:
-            series = series[:1]
-        moves, sums = spread(bent, series)
-        drive.append([mass_head * sums[d][:bond_rows] * flags for d in range(3)])
-        if k < ORDER - 1:
-            square_of.append(
-                [mass_head * sums[3 + 3 * b + a][:bond_rows] * flags for a, b in SYM]
-            )
-            if k == ORDER - 2:
-                series, moves = series[:1], moves[:3]
-            meets = meet(moves)
-            series = [
-                v - bend(bent, meets[3 * i : 3 * i + 3]) for i, v in enumerate(series)
-            ]
+    couplings = [series]
+    for k in range(ORDER - 2):
+        moves, _ = spread(bent, series)
+        meets = meet(moves)
+        series = [v - bend(bent, meets[3 * i : 3 * i + 3]) for i, v in enumerate(series)]
+        couplings.append(series)
+        series = series[:1]
+    once = couplings[1][1:]
+    zero = couplings[0][1:]
+    drive = [[g * couplings[0][0] for g in zero]] + [
+        [g * c[0] for g in once] for c in couplings
+    ]
+    square_of = [
+        [left[a] * other[b] for a, b in SYM]
+        for left, other in ((zero, zero), (once, zero), (once, once))
+    ]
 
     spread_lane = width * sub + entry
 
@@ -400,27 +390,47 @@
             [lanes_at(wide(packed[q][row : row + 1]), spread_lane) for q in range(tiles)], axis=0
         )
 
-    def from_bonds(value):
-        rows = gather(value, bond_tile, bond_lane)
-        return to_rows([rows[q : q + 1] for q in range(tiles)], 0)
-
-    used = from_bonds(jnp.ones((bond_rows, LANES), F32)) > 0.0
-    head_rows = [from_bonds(v) for v in at_head]
-    flat = [v for group in drive + square_of for v in group]
-    flat = to_slots(flat)
-    flat = [
-        to_rows([part[v // SUBS] for part in flat], v % SUBS) for v in range(3 * ORDER + 6 * (ORDER - 1))
-    ]
+    drives = to_slots([v for group in drive + square_of for v in group])
+    places = to_slots([v * flags for v in at_head], 3)
+    for q in range(tiles):
+        for c, part in enumerate(places[q] + drives[q]):
+            out1[c, SUBS * q : SUBS * q + SUBS, :] = transpose8(part)
+    pl.semaphore_wait(barrier, len(greet))
+    hub_first = copies(0, out0, in0, direct, False, False, only=(hub_row,))
+    second = copies(1, out1, in1, forth, True, False, merge=False)
+    others = tuple(row for row in order if row != hub_row)
+    first = copies(0, out0, in0, direct, False, False, only=others)
+
+    entry_rows = jnp.concatenate([entry] * tiles, axis=0)
+    group_rows = jnp.concatenate([group] * tiles, axis=0)
+
+    def packed(values):
+        total = jnp.zeros((SUBS * tiles, LANES), F32)
+        for g, value in enumerate(values):
+            total = jnp.where(group_rows == g, value, total)
+        return total
+
+    def post_terms(values, out):
+        steps = [normal[d] * values[k] for k in range(ORDER + 1) for d in range(3)]
+        post(out, 0, packed(steps[:SUBS]))
+        post(out, 1, packed(steps[SUBS:]))
+
+    arrive(hub_first.values())
+    arrive(second.values())
+    heavy = in0[0, hub_row : hub_row + 1, :] if hub_row != centre else out0[0, 0:1, :]
+    sent_data = [lanes_at(wide(heavy), entry + width * g) for g in range(7)]
+    mass_send = sent_data[6]
+    arrived = [
+        lanes_at(in1[v // SUBS], entry_rows + width * (v % SUBS))
+        for v in range(SUBS + 3 * ORDER + 6 * (ORDER - 1))
+    ]
+    head_rows, flat = arrived[:7], arrived[SUBS:]
     drive = [flat[3 * k : 3 * k + 3] for k in range(ORDER)]
     square_of = [flat[3 * ORDER + 6 * k : 3 * ORDER + 6 * k + 6] for k in range(ORDER - 1)]
-    entry_rows = jnp.concatenate([entry] * tiles, axis=0)
-    group_rows = jnp.concatenate([group] * tiles, axis=0)
-
-    arrive(first)
-    landing = jnp.concatenate(landed(in0, 0), axis=0)
-    tail_rows = [lanes_at(landing, entry_rows + width * g) for g in range(7)]
-    _, _, _, normal, start = geometry(head_rows, tail_rows)
-    normal = [jnp.where(used, b, 0.0) for b in normal]
+    _, _, _, normal, start = geometry(
+        head_rows, [jnp.concatenate([v] * tiles, axis=0) for v in sent_data]
+    )
+    normal = [jnp.where(head_rows[6] > 0.0, b, 0.0) for b in normal]
     pairs = [normal[a] * normal[b] for a, b in SYM]
     keep = 1.0 - head_rows[6] * (pairs[0] + pairs[3] + pairs[5])
     pushes = [
@@ -442,53 +452,22 @@
             value = value + pushes[k - 2 - i] * reply[i]
         reply.append(value)
 
-    def packed(values):
-        total = jnp.zeros((SUBS * tiles, LANES), F32)
-        for g, value in enumerate(values):
-            total = jnp.where(group_rows == g, value, total)
+    def summed(value):
+        total = value[:SUBS]
+        for q in range(1, tiles):
+            total = total + value[SUBS * q : SUBS * q + SUBS]
+        for shift in (4, 2, 1):
+            total = total + pltpu.roll(total, shift, 0)
         return total
 
-    def post_terms(values, out):
-        steps = [normal[d] * values[k] for k in range(ORDER + 1) for d in range(3)]
-        post(out, 0, packed(steps[:SUBS]))
-        post(out, 1, packed(steps[SUBS:]))
-
-    post_terms(chain, out1)
-    quads = [p if reply[g] is None else reply[g] * p for g in range(ORDER) for p in pairs]
-    for c in range(len(quads) // SUBS):
-        post(out1, 2 + c, packed(quads[SUBS * c : SUBS * c + SUBS]))
-    second = copies(1, out1, in1, forth, True, False)
-
-    low = packed([normal[0]] * 4 + [normal[1]] * 4)
-    normal_a = [transpose8(low[SUBS * q : SUBS * q + SUBS]) for q in range(tiles)]
-    normal_b = [
-        transpose8(normal[2][SUBS * q : SUBS * q + SUBS]) for q in range(tiles)
-    ]
-    far = [transpose8(piece) for piece in landed(in0, 0)]
-    at_tail = [jnp.where(is_far, to_bonds(far, g), v) for g, v in enumerate(at_tail)]
-    bond_new, length, scale, bent, right1 = geometry(at_head, at_tail)
-
-    terms, fars = [right1], [flags]
-    term_moves, term_meets, far_moves, far_meets = [], [], [], []
-
-    def advance():
-        moves, _ = spread(bent, [terms[-1], fars[-1]])
-        meets = meet(moves)
-        term_moves.append(moves[:3])
-        far_moves.append(moves[3:])
-        term_meets.append(meets[:3])
-        far_meets.append(meets[3:])
-        terms.append(terms[-1] - bend(bent, meets[:3]))
-        fars.append(fars[-1] - bend(bent, meets[3:]))
-
-    for _ in range(ORDER):
-        advance()
-    last_moves, _ = spread(bent, [terms[ORDER]])
-    last_meets = meet(last_moves)
-    base1 = sum(terms[1:], terms[0])
-
-    arrive(second)
-
+    got = [summed(normal[d] * chain[k]) for k in range(ORDER + 1) for d in range(3)]
+    matrix = [
+        {
+            ab: -mass_send * summed(p if reply[g] is None else reply[g] * p)
+            for ab, p in zip(SYM, pairs)
+        }
+        for g in range(ORDER)
+    ]
     def collect(land):
         found = []
         for part in range(land.shape[0]):
@@ -501,13 +480,6 @@
             for g in range(SUBS):
                 found.append(lanes_at(total, entry + width * g))
         return found
-
-    heavy = in0[0, hub_row : hub_row + 1, :] if hub_row != centre else out0[0, 0:1, :]
-    mass_send = lanes_at(wide(heavy), entry + 6 * width)
-    got = collect(in1)
-    matrix = [
-        {ab: -mass_send * got[2 * SUBS + 6 * g + i] for i, ab in enumerate(SYM)} for g in range(ORDER)
-    ]
 
     def owner(got, out):
         moved = []
@@ -535,6 +507,35 @@
     owner(got, out2)
     third = copies(2, out2, in2, back, False, True)
 
+    arrive(first.values())
+    far = [transpose8(piece) for piece in landed(in0, 0)]
+    at_tail = [jnp.where(is_far, to_bonds(far, g), v) for g, v in enumerate(at_tail)]
+    bond_new, length, scale, bent, right1 = geometry(at_head, at_tail)
+    normal = [part[0] for part in to_slots([b * flags for b in bent])]
+    upper = jnp.where(sub < 4, 0, 1)
+    normal_a = [subs_at(n, upper) for n in normal]
+    normal_b = [wide(n[2:3]) for n in normal]
+    normal = [to_rows(normal, d) for d in range(3)]
+
+    terms, fars = [right1], [flags]
+    term_moves, term_meets, far_moves, far_meets = [], [], [], []
+
+    def advance():
+        moves, _ = spread(bent, [terms[-1], fars[-1]])
+        meets = meet(moves)
+        term_moves.append(moves[:3])
+        far_moves.append(moves[3:])
+        term_meets.append(meets[:3])
+        far_meets.append(meets[3:])
+        terms.append(terms[-1] - bend(bent, meets[:3]))
+        fars.append(fars[-1] - bend(bent, meets[3:]))
+
+    for _ in range(ORDER):
+        advance()
+    last_moves, _ = spread(bent, [terms[ORDER]])
+    last_meets = meet(last_moves)
+    base1 = sum(terms[1:], terms[0])
+
     weights, weight_moves, weight_meets = [], [], []
     for k in range(ORDER):
         if k == 0:
@@ -563,7 +564,7 @@
             total = total + weights[k] * injected[ORDER - 1 - k]
         return total
 
-    arrive(third)
+    arrive(third.values())
     replies1, high = answers(in2)
     injected1 = [to_bonds(replies1, k) for k in range(ORDER)]
     tail_moves = [to_bonds(high, 4 + d) for d in range(3)]
@@ -590,7 +591,7 @@
             term = term - bend(bent, meet(moves))
             both = both + term
         if k == 1:
-            arrive(fourth)
+            arrive(fourth.values())
             owner(collect(in3), out4)
             fifth = copies(4, out4, in4, back, False, True)
 
@@ -618,7 +619,7 @@
     for copy in pending:
         copy.wait_send()
 
-    arrive(fifth)
+    arrive(fifth.values())
     replies2, _ = answers(in4)
     both = both + through(weights, [to_bonds(replies2, k) for k in range(ORDER)])
     mult_ref[0, 0] = both.reshape(1, bonds)

time: 31.2 us -> 27.3 us (0.88)
  Pallas kernels: 29.2 us -> 25.3 us
    pallas_call x1, Pallas kernels: 29.2 us -> 25.3 us  [per_device(): pl.pallas_call(functools.partial(kernel, axes, sizes, send_count), out_sh...]
where the time goes in v3:
time: 27.3 us; the launch traced here: 27.2 us
  Pallas kernels  25.3 us (93%)
  local copies, waits for them, and re-layouts  1.2 us (4%)
  between operations  0.64 us (2%)
    pallas_call x1, Pallas kernels, per_device(): pl.pallas_call(functools.partial(kernel, axes, sizes, send_count), out_sh...  25.3 us
    unnamed x2, local copies, waits for them, and re-layouts  1.2 us

profile of v3, /device:TPU:0, one launch (start us, length us, event | category | flops | bytes accessed | tf_op | source)
XLA Modules:
  0.0 27.2 jit_solution(7994443539492197620)
XLA Ops:
  0.6 25.3 %shard_map.77 = (f32[3,1,1,1,1536]{4,3,2,1,0:T(1,128)S(1)}, f32[1,1,1,1024]{3,2,1,0:T(1,128)S(1)}) custom-call(f32[3,1,1,1,1536]{4,3,2,1,0:T(1,128)} %old_hbm.1, f32[3,1,1,1,1536]{4,3,2,1,0:T(1,128)} %move_hbm.1, f32[1,1,1,1536]{3,2,1,0:T(1,128)} %mass_hbm.1, s32[1,1,1,1024]{3,2,1,0:T(1,128)} %head_hbm.1, s32[1,1,1,1024]{3,2,1,0:T(1,128)} %tail_hbm.1, ...), custom_call_target="tpu_custom_call" | custom-call | tf_op jit(solution)/shard_map/pallas_call | solution.py:650
  25.9 0.6 %copy.10 = f32[3,1,1,1,1536]{4,3,2,1,0:T(1,128)} copy(f32[3,1,1,1,1536]{4,3,2,1,0:T(1,128)S(1)} %get-tuple-element.2) | data formatting | bytes 36864
  26.6 0.6 %copy.11 = f32[1,1,1,1024]{3,2,1,0:T(1,128)} copy(f32[1,1,1,1024]{3,2,1,0:T(1,128)S(1)} %get-tuple-element.3) | data formatting | bytes 8192

commit v4 on v3

--- a/solution.py
+++ b/solution.py
@@ -67,7 +67,7 @@
     old_ref, move_ref, mass_ref, head_ref, tail_ref, send_ref, load_sem,
     table, hot_head, hot_tail, hot_root, mask_tail, mask_root, stage,
     out0, in0, out1, in1, out2, in2, out3, in3, out4, in4,
-    send_sem, recv_sem,
+    spare, send_sem, recv_sem,
 ):
     atoms, bonds = old_ref.shape[-1], head_ref.shape[-1]
     atom_rows, bond_rows = atoms // LANES, bonds // LANES
@@ -307,7 +307,7 @@
     order = sorted(range(len(classes)), key=lambda r: -(classes[r][0] + classes[r][2]))
 
     def copies(step, source, landing, offsets, each, whole, merge=True, only=None):
-        started = {}
+        rows = 0
         for row in only or order:
             if row == centre and not whole or merge and twin and classes[row][1] == 2:
                 continue
@@ -317,12 +317,12 @@
                 continue
             copy = pltpu.make_async_remote_copy(
                 source.at[:, line], landing.at[:, row],
-                send_sem.at[step, row], recv_sem.at[step, row],
+                send_sem.at[step], recv_sem.at[step],
                 device_id=target(offsets[row]), device_id_type=MESH,
             )
             copy.start()
-            started[row] = copy
-        return started
+            rows += source.shape[0]
+        return step, rows
 
     def post(out, part, value):
         pieces = [value[SUBS * q : SUBS * q + SUBS] for q in range(tiles)]
@@ -342,10 +342,15 @@
 
     pending = []
 
+    def drain(sem, rows):
+        lines = spare.at[pl.ds(0, rows)]
+        pltpu.make_async_copy(lines, lines, sem).wait()
+
     def arrive(started):
-        for copy in started:
-            copy.wait_recv()
-            pending.append(copy)
+        step, rows = started
+        if rows:
+            drain(recv_sem.at[step], rows)
+            pending.append(started)
 
 
     mass_head = at_head[6]
@@ -396,7 +401,7 @@
         for c, part in enumerate(places[q] + drives[q]):
             out1[c, SUBS * q : SUBS * q + SUBS, :] = transpose8(part)
     pl.semaphore_wait(barrier, len(greet))
-    hub_first = copies(0, out0, in0, direct, False, False, only=(hub_row,))
+    hub_first = copies(5, out0, in0, direct, False, False, only=(hub_row,))
     second = copies(1, out1, in1, forth, True, False, merge=False)
     others = tuple(row for row in order if row != hub_row)
     first = copies(0, out0, in0, direct, False, False, only=others)
@@ -415,8 +420,8 @@
         post(out, 0, packed(steps[:SUBS]))
         post(out, 1, packed(steps[SUBS:]))
 
-    arrive(hub_first.values())
-    arrive(second.values())
+    arrive(hub_first)
+    arrive(second)
     heavy = in0[0, hub_row : hub_row + 1, :] if hub_row != centre else out0[0, 0:1, :]
     sent_data = [lanes_at(wide(heavy), entry + width * g) for g in range(7)]
     mass_send = sent_data[6]
@@ -507,7 +512,7 @@
     owner(got, out2)
     third = copies(2, out2, in2, back, False, True)
 
-    arrive(first.values())
+    arrive(first)
     far = [transpose8(piece) for piece in landed(in0, 0)]
     at_tail = [jnp.where(is_far, to_bonds(far, g), v) for g, v in enumerate(at_tail)]
     bond_new, length, scale, bent, right1 = geometry(at_head, at_tail)
@@ -564,7 +569,7 @@
             total = total + weights[k] * injected[ORDER - 1 - k]
         return total
 
-    arrive(third.values())
+    arrive(third)
     replies1, high = answers(in2)
     injected1 = [to_bonds(replies1, k) for k in range(ORDER)]
     tail_moves = [to_bonds(high, 4 + d) for d in range(3)]
@@ -591,7 +596,7 @@
             term = term - bend(bent, meet(moves))
             both = both + term
         if k == 1:
-            arrive(fourth.values())
+            arrive(fourth)
             owner(collect(in3), out4)
             fifth = copies(4, out4, in4, back, False, True)
 
@@ -616,10 +621,10 @@
         for w in weight_moves
     ]
     early = len(pending)
-    for copy in pending:
-        copy.wait_send()
-
-    arrive(fifth.values())
+    for step, rows in pending:
+        drain(send_sem.at[step], rows)
+
+    arrive(fifth)
     replies2, _ = answers(in4)
     both = both + through(weights, [to_bonds(replies2, k) for k in range(ORDER)])
     mult_ref[0, 0] = both.reshape(1, bonds)
@@ -637,8 +642,8 @@
         result = at_atoms[d] - through([w[d] for w in weight_moves], injected)
         result = result - jnp.where(sent, lanes_at(own, entry_of + width * (4 + d)), 0.0)
         pos_ref[d, 0, 0] = result.reshape(1, atoms)
-    for copy in pending[early:]:
-        copy.wait_send()
+    for step, rows in pending[early:]:
+        drain(send_sem.at[step], rows)
 
 
 def per_device(axes, sizes, old_pos, displacement, inv_mass, bond_head, bond_tail, send_list):
@@ -669,8 +674,9 @@
             vmem(2, SUBS), vmem(2, rows),
             vmem(2, rows), vmem(2, rows),
             vmem(2, SUBS), vmem(2, rows),
-            pltpu.SemaphoreType.DMA((5, 27)),
-            pltpu.SemaphoreType.DMA((5, 27)),
+            vmem(5 * rows),
+            pltpu.SemaphoreType.DMA((6,)),
+            pltpu.SemaphoreType.DMA((6,)),
         ],
         compiler_params=pltpu.CompilerParams(
             collective_id=0, has_side_effects=True, vmem_limit_bytes=56 * 1024 * 1024

time: 27.3 us -> 24.9 us (0.912)
  Pallas kernels: 25.3 us -> 22.9 us
    pallas_call x1, Pallas kernels: 25.3 us -> 22.9 us  [per_device(): pl.pallas_call(functools.partial(kernel, axes, sizes, send_count), out_sh...]
where the time goes in v4:
time: 24.9 us; the launch traced here: 24.7 us
  Pallas kernels  22.9 us (92%)
  local copies, waits for them, and re-layouts  1.2 us (5%)
  between operations  0.64 us (3%)
    pallas_call x1, Pallas kernels, per_device(): pl.pallas_call(functools.partial(kernel, axes, sizes, send_count), out_sh...  22.9 us
    unnamed x2, local copies, waits for them, and re-layouts  1.2 us

profile of v4, /device:TPU:0, one launch (start us, length us, event | category | flops | bytes accessed | tf_op | source)
XLA Modules:
  0.0 24.7 jit_solution(6048252241360875963)
XLA Ops:
  0.6 22.9 %shard_map.77 = (f32[3,1,1,1,1536]{4,3,2,1,0:T(1,128)S(1)}, f32[1,1,1,1024]{3,2,1,0:T(1,128)S(1)}) custom-call(f32[3,1,1,1,1536]{4,3,2,1,0:T(1,128)} %old_hbm.1, f32[3,1,1,1,1536]{4,3,2,1,0:T(1,128)} %move_hbm.1, f32[1,1,1,1536]{3,2,1,0:T(1,128)} %mass_hbm.1, s32[1,1,1,1024]{3,2,1,0:T(1,128)} %head_hbm.1, s32[1,1,1,1024]{3,2,1,0:T(1,128)} %tail_hbm.1, ...), custom_call_target="tpu_custom_call" | custom-call | tf_op jit(solution)/shard_map/pallas_call | solution.py:655
  23.5 0.6 %copy.10 = f32[3,1,1,1,1536]{4,3,2,1,0:T(1,128)} copy(f32[3,1,1,1,1536]{4,3,2,1,0:T(1,128)S(1)} %get-tuple-element.2) | data formatting | bytes 36864
  24.2 0.6 %copy.11 = f32[1,1,1,1024]{3,2,1,0:T(1,128)} copy(f32[1,1,1,1024]{3,2,1,0:T(1,128)S(1)} %get-tuple-element.3) | data formatting | bytes 8192

commit v5 on v4

--- a/solution.py
+++ b/solution.py
@@ -52,12 +52,11 @@
     plane = [(a, c) for a in range(3) for c in range(3)]
     classes = [(a, b, c) for b in (0, 2, 1) for a, c in plane[:SUBS]]
     classes += [plane[SUBS][:1] + (b,) + plane[SUBS][1:] for b in (0, 2, 1)]
-    direct, forth, back = [], [], []
+    forth, back = [], []
     for cls in classes:
-        direct.append(tuple((1 - c) for c in cls))
         forth.append(tuple((0, 1, -2)[c] if flips(n) else c - 1 for c, n in zip(cls, sizes)))
         back.append(tuple((0, 1, 2)[c] if flips(n) else 1 - c for c, n in zip(cls, sizes)))
-    return classes, direct, forth, back
+    return classes, forth, back
 
 
 def kernel(
@@ -65,8 +64,8 @@
     old_hbm, move_hbm, mass_hbm, head_hbm, tail_hbm, send_hbm,
     pos_ref, mult_ref,
     old_ref, move_ref, mass_ref, head_ref, tail_ref, send_ref, load_sem,
-    table, hot_head, hot_tail, hot_root, mask_tail, mask_root, stage,
-    out0, in0, out1, in1, out2, in2, out3, in3, out4, in4,
+    table, hot_head, hot_tail, hot_tree, hot_root, mask_tail, mask_tree, mask_root, stage,
+    out0, held, in0, out1, in1, out2, in2, out3, in3, out4, in4,
     spare, send_sem, recv_sem,
 ):
     atoms, bonds = old_ref.shape[-1], head_ref.shape[-1]
@@ -74,9 +73,8 @@
     slot_rows = bond_rows + -(-(atoms - bonds) // LANES)
     width = send_count
     bits = width.bit_length() - 1
-    classes, direct, forth, back = routes(sizes)
+    classes, forth, back = routes(sizes)
     centre = classes.index((1, 1, 1))
-    hub_row = classes.index(tuple(0 if flips(n) else 1 for n in sizes))
     tiles = -(-len(classes) // SUBS)
     here = [lax.axis_index(name) for name in axes]
     turn = [1 - 2 * lax.rem(i, 2) if flips(n) else 1 for i, n in zip(here, sizes)]
@@ -92,7 +90,7 @@
         )
 
     greet = []
-    for group in (direct, forth, back):
+    for group in (forth, back):
         for offset in group:
             key = tuple(o % n for o, n in zip(offset, sizes))
             if any(key) and key not in [k for k, _ in greet]:
@@ -127,28 +125,6 @@
     old = [old_ref[k, 0, 0].reshape(atom_rows, LANES) for k in range(3)]
     pos0 = [old[k] + move_ref[k, 0, 0].reshape(atom_rows, LANES) for k in range(3)]
     mass = mass_ref[0, 0].reshape(atom_rows, LANES)
-    values = old + pos0 + [mass, jnp.zeros((atom_rows, LANES), F32)]
-    for g, value in enumerate(values):
-        for q in range(atom_rows):
-            table[SUBS * q + g : SUBS * q + g + 1, :] = value[q : q + 1]
-    send_row = jnp.concatenate(
-        [send_ref[0, 0], jnp.zeros((1, LANES - send_count), I32)], axis=1
-    )
-    send_rep = lanes_at(wide(send_row), entry)
-    send_tile, send_lane = lax.shift_right_logical(send_rep, 7), send_rep & (LANES - 1)
-    found = jnp.zeros((SUBS, LANES), F32)
-    for q in range(atom_rows):
-        found = jnp.where(
-            send_tile == q, lanes_at(table[SUBS * q : SUBS * q + SUBS, :], send_lane), found
-        )
-    found = jnp.sum(jnp.where(group == sub, found, 0.0), axis=0, keepdims=True)
-    out0[0] = wide(found)
-    for land in (in1, in3):
-        for part in range(land.shape[0]):
-            land[part, centre : centre + 1, :] = jnp.zeros((1, LANES), F32)
-            land[part, len(classes) :, :] = jnp.zeros((SUBS * tiles - len(classes), LANES), F32)
-            if twin and land is in3:
-                land[part, 3 * SUBS + 1 : 3 * SUBS + 2, :] = jnp.zeros((1, LANES), F32)
     head = head_ref[0, 0].reshape(bond_rows, LANES)
     tail = tail_ref[0, 0].reshape(bond_rows, LANES)
     head_tile, head_lane = lax.shift_right_logical(head, 7), head & (LANES - 1)
@@ -194,19 +170,13 @@
         ).astype(BF16))
     owner_of = dot_nt(jnp.concatenate(parts, axis=1), hot_head[...])
     owner_of = owner_of[:16] + owner_of[16:]
-    free = jnp.where(owner_of == 0.0, 1.0, 0.0).astype(BF16)
-    before = dot_nn(free, jnp.where(deep < across, 1.0, 0.0).astype(BF16))
-    totals = dot_nn(free, jnp.ones((LANES, LANES), BF16))
-    for q in range(atom_rows - 1):
-        before = before + jnp.where(row16 > q, wide(totals[q : q + 1], 16), 0.0)
-    place_of = jnp.where(owner_of > 0.0, owner_of - 1.0, before + float(bonds)).astype(I32)
-    spot = gather(place_of, tail_tile, tail_lane, 0, atom_rows)
-    spot = jnp.where(is_far, -1, spot)
-    spot_tile, spot_lane = lax.shift_right_arithmetic(spot, 7), spot & (LANES - 1)
+    tree = gather(owner_of, tail_tile, tail_lane, 0.0, atom_rows).astype(I32) - 1
+    tree = jnp.where(is_far, -1, tree)
+    tree_tile, tree_lane = lax.shift_right_arithmetic(tree, 7), tree & (LANES - 1)
 
     label = jnp.where(is_far, slot, -1)
     for _ in range(ORDER + 1):
-        label = jnp.where(is_far, slot, gather(label, spot_tile, spot_lane, -1))
+        label = jnp.where(is_far, slot, gather(label, tree_tile, tree_lane, -1))
     label_tile, label_lane = lax.shift_right_arithmetic(label, 7), label & (LANES - 1)
 
     def columns(index, dest):
@@ -217,11 +187,11 @@
                 col[:, s : s + 1] == line, 1.0, 0.0
             ).astype(BF16)
 
-    columns(spot_lane, hot_tail)
+    columns(tree_lane, hot_tree)
     columns(label_lane, hot_root)
     for s in range(bond_rows):
-        mask_tail[16 * s : 16 * s + 16, :] = jnp.where(
-            row16 == wide(spot_tile[s : s + 1], 16), 1.0, 0.0
+        mask_tree[16 * s : 16 * s + 16, :] = jnp.where(
+            (row16 & (SUBS - 1)) == wide(tree_tile[s : s + 1], 16), 1.0, 0.0
         ).astype(BF16)
         for q in range(tiles):
             base = 16 * (s * tiles + q)
@@ -250,7 +220,26 @@
         return [
             jnp.concatenate([p - t[:bond_rows], -t[bond_rows:slot_rows]], axis=0)
             for p, t in zip(pulls, sums)
-        ], sums
+        ]
+
+    def spread_tree(bent, rows):
+        pulls = [bent[d] * row for row in rows for d in range(3)]
+        halves = [split(pull) for pull in pulls]
+        parts = []
+        for s in range(bond_rows):
+            mask = mask_tree[16 * s : 16 * s + 16, :]
+            parts.append(jnp.concatenate([
+                jnp.concatenate([wide(half[s : s + 1]) for half in pair], axis=0).astype(BF16) * mask
+                for pair in halves
+            ], axis=0))
+        out = dot_nn(jnp.concatenate(parts, axis=1), hot_tree[...])
+        return [
+            pull - (out[16 * i : 16 * i + 8] + out[16 * i + 8 : 16 * i + 16])
+            for i, pull in enumerate(pulls)
+        ]
+
+    def meet_tree(moves):
+        return [mass_head * m - near_mass * gather(m, tree_tile, tree_lane) for m in moves]
 
     def meet(moves):
         return [
@@ -304,11 +293,14 @@
         return total
 
     flags = jnp.where(is_far, 1.0, 0.0)
-    order = sorted(range(len(classes)), key=lambda r: -(classes[r][0] + classes[r][2]))
-
-    def copies(step, source, landing, offsets, each, whole, merge=True, only=None):
+    order = sorted(
+        range(len(classes)),
+        key=lambda r: -(4 * min(classes[r][0], 1) + 4 * classes[r][2] + abs(classes[r][1] - 1)),
+    )
+
+    def copies(step, source, landing, offsets, each, whole, merge=True):
         rows = 0
-        for row in only or order:
+        for row in order:
             if row == centre and not whole or merge and twin and classes[row][1] == 2:
                 continue
             line = row if each else 0
@@ -366,16 +358,24 @@
         )
         return news, size, scale, [scale * d for d in direction], right
 
-    _, _, _, bent, right = geometry(at_head, at_tail)
-    bent = [jnp.where(is_far, 0.0, b) for b in bent]
+    near_new, near_length, near_scale, near, right = geometry(at_head, at_tail)
+    near = [jnp.where(is_far, 0.0, b) for b in near]
     near_mass = jnp.where(is_far, 0.0, at_tail[6])
-    kids = gather(flags, spot_tile, spot_lane) * near_mass
-    series = [jnp.where(is_far, 0.0, right)] + [kids * b for b in bent]
+    kids = gather(flags, tree_tile, tree_lane) * near_mass
+    series = [jnp.where(is_far, 0.0, right)] + [kids * b for b in near]
+
+    def advance(series, spread=spread_tree, meet=meet_tree):
+        moves = spread(near, series)
+        meets = meet(moves)
+        return [
+            v - bend(near, meets[3 * i : 3 * i + 3]) for i, v in enumerate(series)
+        ], moves, meets
+
     couplings = [series]
     for k in range(ORDER - 2):
-        moves, _ = spread(bent, series)
-        meets = meet(moves)
-        series = [v - bend(bent, meets[3 * i : 3 * i + 3]) for i, v in enumerate(series)]
+        series, moves, meets = advance(series)
+        if k == 0:
+            unit_moves, unit_meets = [moves[3:]], [meets[3:]]
         couplings.append(series)
         series = series[:1]
     once = couplings[1][1:]
@@ -401,10 +401,94 @@
         for c, part in enumerate(places[q] + drives[q]):
             out1[c, SUBS * q : SUBS * q + SUBS, :] = transpose8(part)
     pl.semaphore_wait(barrier, len(greet))
-    hub_first = copies(5, out0, in0, direct, False, False, only=(hub_row,))
     second = copies(1, out1, in1, forth, True, False, merge=False)
-    others = tuple(row for row in order if row != hub_row)
-    first = copies(0, out0, in0, direct, False, False, only=others)
+
+    values = old + pos0 + [mass, jnp.zeros((atom_rows, LANES), F32)]
+    for g, value in enumerate(values):
+        for q in range(atom_rows):
+            table[SUBS * q + g : SUBS * q + g + 1, :] = value[q : q + 1]
+    send_row = jnp.concatenate(
+        [send_ref[0, 0], jnp.zeros((1, LANES - send_count), I32)], axis=1
+    )
+    send_rep = lanes_at(wide(send_row), entry)
+    send_tile, send_lane = lax.shift_right_logical(send_rep, 7), send_rep & (LANES - 1)
+    found = jnp.zeros((SUBS, LANES), F32)
+    for q in range(atom_rows):
+        found = jnp.where(
+            send_tile == q, lanes_at(table[SUBS * q : SUBS * q + SUBS, :], send_lane), found
+        )
+    found = jnp.sum(jnp.where(group == sub, found, 0.0), axis=0, keepdims=True)
+    out0[0] = wide(found)
+    for land in (in1, in3):
+        for part in range(land.shape[0]):
+            land[part, centre : centre + 1, :] = jnp.zeros((1, LANES), F32)
+            land[part, len(classes) :, :] = jnp.zeros((SUBS * tiles - len(classes), LANES), F32)
+            if twin and land is in3:
+                land[part, 3 * SUBS + 1 : 3 * SUBS + 2, :] = jnp.zeros((1, LANES), F32)
+    if nowhere(forth[centre]):
+        to_hub = 5, 0
+        held[...] = out0[...]
+    else:
+        pltpu.make_async_remote_copy(
+            out0.at[:, 0], held.at[:, 0], send_sem.at[5], recv_sem.at[5],
+            device_id=target(forth[centre]), device_id_type=MESH,
+        ).start()
+        to_hub = 5, 1
+
+    free = jnp.where(owner_of == 0.0, 1.0, 0.0).astype(BF16)
+    before = dot_nn(free, jnp.where(deep < across, 1.0, 0.0).astype(BF16))
+    totals = dot_nn(free, jnp.ones((LANES, LANES), BF16))
+    for q in range(atom_rows - 1):
+        before = before + jnp.where(row16 > q, wide(totals[q : q + 1], 16), 0.0)
+    place_of = jnp.where(owner_of > 0.0, owner_of - 1.0, before + float(bonds)).astype(I32)
+    spot = gather(place_of, tail_tile, tail_lane, 0, atom_rows)
+    spot = jnp.where(is_far, -1, spot)
+    spot_tile, spot_lane = lax.shift_right_arithmetic(spot, 7), spot & (LANES - 1)
+    columns(spot_lane, hot_tail)
+    for s in range(bond_rows):
+        mask_tail[16 * s : 16 * s + 16, :] = jnp.where(
+            row16 == wide(spot_tile[s : s + 1], 16), 1.0, 0.0
+        ).astype(BF16)
+
+    def powers(normal, mass_at, start, drive, square_of, last):
+        pairs = [normal[a] * normal[b] for a, b in SYM]
+        keep = 1.0 - mass_at * (pairs[0] + pairs[3] + pairs[5])
+        pushes = [
+            q[0] * pairs[0] + q[3] * pairs[3] + q[5] * pairs[5]
+            + 2.0 * (q[1] * pairs[1] + q[2] * pairs[2] + q[4] * pairs[4])
+            for q in square_of
+        ]
+        chain, reply = [start], [None, keep]
+        for k in range(1, ORDER + 1):
+            value = keep * chain[-1] + bend(normal, drive[k - 1])
+            for i in range(k - 1):
+                value = value + pushes[k - 2 - i] * chain[i]
+            chain.append(value)
+        for k in range(2, last + 1):
+            value = keep * reply[-1] + pushes[k - 2]
+            for i in range(1, k - 1):
+                value = value + pushes[k - 2 - i] * reply[i]
+            reply.append(value)
+        return pairs, chain, reply
+
+    units = [zero, once]
+    rights = [couplings[0][0]]
+    for k in range(ORDER):
+        series, _, _ = advance(rights[-1:], spread, meet)
+        rights += series
+        if k:
+            series, moves, meets = advance(units[k])
+            unit_moves.append(moves)
+            unit_meets.append(meets)
+            units.append(series)
+    near_sum = sum(rights[1:], rights[0])
+    near_moves = spread(near, [near_sum])
+    near_meets = meet(near_moves)
+    root_head = [to_bonds([part[0] for part in places], g) for g in range(7)]
+    root_flat = [
+        to_bonds([part[v // SUBS] for part in drives], v % SUBS)
+        for v in range(3 * ORDER + 6 * (ORDER - 1))
+    ]
 
     entry_rows = jnp.concatenate([entry] * tiles, axis=0)
     group_rows = jnp.concatenate([group] * tiles, axis=0)
@@ -420,10 +504,10 @@
         post(out, 0, packed(steps[:SUBS]))
         post(out, 1, packed(steps[SUBS:]))
 
-    arrive(hub_first)
+    arrive(to_hub)
+    first = copies(0, held, in0, back, False, False)
     arrive(second)
-    heavy = in0[0, hub_row : hub_row + 1, :] if hub_row != centre else out0[0, 0:1, :]
-    sent_data = [lanes_at(wide(heavy), entry + width * g) for g in range(7)]
+    sent_data = [lanes_at(wide(held[0, 0:1, :]), entry + width * g) for g in range(7)]
     mass_send = sent_data[6]
     arrived = [
         lanes_at(in1[v // SUBS], entry_rows + width * (v % SUBS))
@@ -436,26 +520,7 @@
         head_rows, [jnp.concatenate([v] * tiles, axis=0) for v in sent_data]
     )
     normal = [jnp.where(head_rows[6] > 0.0, b, 0.0) for b in normal]
-    pairs = [normal[a] * normal[b] for a, b in SYM]
-    keep = 1.0 - head_rows[6] * (pairs[0] + pairs[3] + pairs[5])
-    pushes = [
-        q[0] * pairs[0] + q[3] * pairs[3] + q[5] * pairs[5]
-        + 2.0 * (q[1] * pairs[1] + q[2] * pairs[2] + q[4] * pairs[4])
-        for q in square_of
-    ]
-    chain, reply = [start], [None, keep]
-    for k in range(1, ORDER + 1):
-        value = keep * chain[-1] + (
-            normal[0] * drive[k - 1][0] + normal[1] * drive[k - 1][1] + normal[2] * drive[k - 1][2]
-        )
-        for i in range(k - 1):
-            value = value + pushes[k - 2 - i] * chain[i]
-        chain.append(value)
-    for k in range(2, ORDER):
-        value = keep * reply[-1] + pushes[k - 2]
-        for i in range(1, k - 1):
-            value = value + pushes[k - 2 - i] * reply[i]
-        reply.append(value)
+    pairs, chain, reply = powers(normal, head_rows[6], start, drive, square_of, ORDER - 1)
 
     def summed(value):
         total = value[:SUBS]
@@ -514,32 +579,73 @@
 
     arrive(first)
     far = [transpose8(piece) for piece in landed(in0, 0)]
-    at_tail = [jnp.where(is_far, to_bonds(far, g), v) for g, v in enumerate(at_tail)]
-    bond_new, length, scale, bent, right1 = geometry(at_head, at_tail)
-    normal = [part[0] for part in to_slots([b * flags for b in bent])]
+    root_new, root_length, root_scale, root, start = geometry(
+        root_head, [to_bonds(far, g) for g in range(7)]
+    )
+    rooted = label >= 0
+    root = [jnp.where(rooted, b, 0.0) for b in root]
+    normal = [part[0] for part in to_slots([b * flags for b in root])]
     upper = jnp.where(sub < 4, 0, 1)
     normal_a = [subs_at(n, upper) for n in normal]
     normal_b = [wide(n[2:3]) for n in normal]
     normal = [to_rows(normal, d) for d in range(3)]
 
-    terms, fars = [right1], [flags]
-    term_moves, term_meets, far_moves, far_meets = [], [], [], []
-
-    def advance():
-        moves, _ = spread(bent, [terms[-1], fars[-1]])
-        meets = meet(moves)
-        term_moves.append(moves[:3])
-        far_moves.append(moves[3:])
-        term_meets.append(meets[:3])
-        far_meets.append(meets[3:])
-        terms.append(terms[-1] - bend(bent, meets[:3]))
-        fars.append(fars[-1] - bend(bent, meets[3:]))
-
-    for _ in range(ORDER):
-        advance()
-    last_moves, _ = spread(bent, [terms[ORDER]])
-    last_meets = meet(last_moves)
-    base1 = sum(terms[1:], terms[0])
+    _, chain, reply = powers(
+        root, root_head[6], jnp.where(rooted, start, 0.0),
+        [root_flat[3 * k : 3 * k + 3] for k in range(ORDER)],
+        [root_flat[3 * ORDER + 6 * k : 3 * ORDER + 6 * k + 6] for k in range(ORDER - 1)], ORDER,
+    )
+    reply[0] = jnp.ones((bond_rows, LANES), F32)
+    bond_new = [jnp.where(is_far, a, b) for a, b in zip(root_new, near_new)]
+    length = jnp.where(is_far, root_length, near_length)
+    scale = jnp.where(is_far, root_scale, near_scale)
+    bent = [jnp.where(is_far, a, b) for a, b in zip(root, near)]
+    own_meet = flags * mass_head - kids
+
+    def rooted_sum(part):
+        return [
+            sum([root[e] * part[3 * e + d][:bond_rows] for e in (1, 2)], root[0] * part[d][:bond_rows])
+            for d in range(3)
+        ]
+
+    unit_sums = [bend(root, unit) for unit in units[:ORDER]]
+    unit_moves = [rooted_sum(part) for part in unit_moves]
+    unit_meets = [rooted_sum(part) for part in unit_meets]
+
+    def combine(first, factors, parts):
+        for factor, part in zip(factors, parts):
+            first = first + factor * part
+        return first
+
+    fars, far_moves, far_meets = [], [], []
+    for k in range(ORDER + 1):
+        back_k = reply[:k][::-1]
+        fars.append(combine(flags * reply[k], back_k, unit_sums))
+        far_moves.append([
+            combine(flags * reply[k] * root[d], back_k, [m[d] for m in unit_moves]) for d in range(3)
+        ])
+        far_meets.append([
+            combine(own_meet * reply[k] * root[d], back_k, [m[d] for m in unit_meets])
+            for d in range(3)
+        ])
+    totals = [chain[0]]
+    for k in range(1, ORDER + 1):
+        totals.append(totals[-1] + chain[k])
+    back_k = totals[:ORDER][::-1]
+    base1 = near_sum + combine(flags * totals[ORDER], back_k, unit_sums)
+    base_moves = [
+        jnp.concatenate([
+            near_moves[d][:bond_rows]
+            + combine(flags * totals[ORDER] * root[d], back_k, [m[d] for m in unit_moves]),
+            near_moves[d][bond_rows:],
+        ], axis=0)
+        for d in range(3)
+    ]
+    base_meets = [
+        near_meets[d]
+        + combine(own_meet * totals[ORDER] * root[d], back_k, [m[d] for m in unit_meets])
+        for d in range(3)
+    ]
 
     weights, weight_moves, weight_meets = [], [], []
     for k in range(ORDER):
@@ -551,9 +657,6 @@
             weights.append(weights[-1] + fars[k])
             weight_moves.append([a + b for a, b in zip(weight_moves[-1], far_moves[k])])
             weight_meets.append([a + b for a, b in zip(weight_meets[-1], far_meets[k])])
-    base_moves = [sum([m[d] for m in term_moves], last_moves[d]) for d in range(3)]
-    base_meets = [sum([m[d] for m in term_meets], last_meets[d]) for d in range(3)]
-
     def answers(land):
         low = [transpose8(piece) for piece in landed(land, 0)]
         high = [transpose8(piece) for piece in landed(land, 1)]
@@ -590,7 +693,7 @@
 
     term, both = right2, sol1 + right2
     for k in range(ORDER + 1):
-        moves, _ = spread(bent, [term])
+        moves = spread(bent, [term])
         base_moves = [a + b for a, b in zip(base_moves, moves)]
         if k < ORDER:
             term = term - bend(bent, meet(moves))
@@ -666,10 +769,11 @@
             pltpu.VMEM(bond_tail.shape, I32), pltpu.VMEM(send_list.shape, I32),
             pltpu.SemaphoreType.DMA((6,)),
             vmem(atoms // LANES * SUBS),
-            half(LANES, bonds), half(bonds, LANES), half(bonds, LANES),
-            half(16 * bond_rows, LANES), half(16 * bond_rows * 4, LANES),
+            half(LANES, bonds), half(bonds, LANES), half(bonds, LANES), half(bonds, LANES),
+            half(16 * bond_rows, LANES), half(16 * bond_rows, LANES),
+            half(16 * bond_rows * 4, LANES),
             vmem(4 * SUBS * SUBS),
-            vmem(1, SUBS), vmem(1, rows),
+            vmem(1, SUBS), vmem(1, SUBS), vmem(1, rows),
             vmem(5, rows), vmem(5, rows),
             vmem(2, SUBS), vmem(2, rows),
             vmem(2, rows), vmem(2, rows),

time: 24.9 us -> 24.7 us (level)
  no operation moved by 1% of the time
where the time goes in v5:
time: 24.7 us; the launch traced here: 24.5 us
  Pallas kernels  22.7 us (92%)
  local copies, waits for them, and re-layouts  1.2 us (5%)
  between operations  0.64 us (3%)
    pallas_call x1, Pallas kernels, per_device(): pl.pallas_call(functools.partial(kernel, axes, sizes, send_count), out_sh...  22.7 us
    unnamed x2, local copies, waits for them, and re-layouts  1.2 us

profile of v5, /device:TPU:0, one launch (start us, length us, event | category | flops | bytes accessed | tf_op | source)
XLA Modules:
  0.0 24.5 jit_solution(13139797649350139409)
XLA Ops:
  0.6 22.7 %shard_map.77 = (f32[3,1,1,1,1536]{4,3,2,1,0:T(1,128)S(1)}, f32[1,1,1,1024]{3,2,1,0:T(1,128)S(1)}) custom-call(f32[3,1,1,1,1536]{4,3,2,1,0:T(1,128)} %old_hbm.1, f32[3,1,1,1,1536]{4,3,2,1,0:T(1,128)} %move_hbm.1, f32[1,1,1,1536]{3,2,1,0:T(1,128)} %mass_hbm.1, s32[1,1,1,1024]{3,2,1,0:T(1,128)} %head_hbm.1, s32[1,1,1,1024]{3,2,1,0:T(1,128)} %tail_hbm.1, ...), custom_call_target="tpu_custom_call" | custom-call | tf_op jit(solution)/shard_map/pallas_call | solution.py:758
  23.3 0.6 %copy.10 = f32[3,1,1,1,1536]{4,3,2,1,0:T(1,128)} copy(f32[3,1,1,1,1536]{4,3,2,1,0:T(1,128)S(1)} %get-tuple-element.2) | data formatting | bytes 36864
  23.9 0.6 %copy.11 = f32[1,1,1,1024]{3,2,1,0:T(1,128)} copy(f32[1,1,1,1024]{3,2,1,0:T(1,128)S(1)} %get-tuple-element.3) | data formatting | bytes 8192
